TPU v7x, 64 devices: a 2x2x8 block of a 4x4x8 slice. The times are simulated.
64 devices in a mesh: dp: 4 (over x, y), ep: 16 (over z, core).
Axes of the slice: x: 2, y: 2, z: 8, core: 2. Of those that a mesh axis runs over, the one named last changes fastest.
The devices are a block of a 4x4x8 slice.
Arguments:
- tokens: bfloat16 [8192, 2048], P(('dp', 'ep')), parts along dimension 0
- topk_idx: int32 [8192, 8], P(('dp', 'ep')), parts along dimension 0
- topk_w: float32 [8192, 8], P(('dp', 'ep')), parts along dimension 0
- w_up: bfloat16 [16, 9, 2048, 768], P('ep')
- w_down: bfloat16 [16, 9, 768, 2048], P('ep')
- slot_expert: int32 [16, 9], replicated
Outputs:
- output: bfloat16 [8192, 2048], P(('dp', 'ep')), parts along dimension 0
There are 4 independent parts. A program takes and returns all parts, laid end to end along the dimension named above; an argument that names none is the same for every part.
All inputs are finite; a program needn't handle non-finite values.
Results may differ from a plain program's by a relative error of at most 0.0013.
Values are sent between devices in bfloat16 or wider.
A program may use at most 768 MiB of HBM per device.

v0:
```python
import jax
import jax.numpy as jnp
from jax import lax
from jax.sharding import PartitionSpec as P

MAX_COPIES = 4


def slot_bound(n_tok, n_top, n_dev, n_slot):
    base_load = (n_tok * n_top) // (n_dev * n_slot)
    return base_load + base_load // 2 + 1


def route_pairs(topk_idx, slot_expert, capacity):
    n_dev, n_slot = slot_expert.shape
    n_exp = n_dev * (n_slot - 1)
    n_top = topk_idx.shape[1]
    table_flat = slot_expert.reshape(-1)
    slot_ids = jnp.arange(n_dev * n_slot, dtype=jnp.int32)
    same_exp = table_flat[:, None] == table_flat[None, :]
    earlier = slot_ids[None, :] < slot_ids[:, None]
    copy_rank = jnp.sum(same_exp & earlier, axis=1, dtype=jnp.int32)
    exp_copies = jax.ops.segment_sum(jnp.ones_like(table_flat), table_flat, num_segments=n_exp)
    slot_of = jnp.zeros((n_exp, MAX_COPIES), jnp.int32).at[table_flat, copy_rank].set(slot_ids)
    flat_exp = topk_idx.reshape(-1)
    onehot = (flat_exp[:, None] == jnp.arange(n_exp, dtype=jnp.int32)[None, :]).astype(jnp.int32)
    pair_rank = jnp.sum((jnp.cumsum(onehot, axis=0) - onehot) * onehot, axis=1)
    pair_copies = exp_copies[flat_exp]
    slot_flat = slot_of[flat_exp, pair_rank % pair_copies]
    buf_row = pair_rank // pair_copies
    pair_pos = ((slot_flat % n_slot) * n_dev + slot_flat // n_slot) * capacity + buf_row
    pair_tok = jnp.arange(flat_exp.shape[0], dtype=jnp.int32) // n_top
    buf_tok = jnp.zeros((n_slot * n_dev * capacity,), jnp.int32).at[pair_pos].set(pair_tok)
    return pair_pos, buf_tok


def expert_ffn(recv_buf, up_local, down_local):
    pre_act = jnp.einsum('spcm,smf->spcf', recv_buf, up_local, preferred_element_type=jnp.float32)
    hidden = jax.nn.gelu(pre_act, approximate=True).astype(jnp.bfloat16)
    return jnp.einsum('spcf,sfm->spcm', hidden, down_local, preferred_element_type=jnp.float32).astype(jnp.bfloat16)


def solution(mesh):
    def group_layer(tokens, topk_idx, topk_w, w_up, w_down, slot_expert):
        n_tok, d_model = tokens.shape
        n_top = topk_idx.shape[1]
        n_dev, n_slot = slot_expert.shape
        capacity = slot_bound(n_tok, n_top, n_dev, n_slot)
        pair_pos, buf_tok = route_pairs(topk_idx, slot_expert, capacity)
        send_buf = tokens[buf_tok].reshape(n_slot, n_dev, capacity, d_model)
        recv_buf = lax.all_to_all(send_buf, 'ep', 1, 1, tiled=True)
        expert_out = expert_ffn(recv_buf, w_up[0], w_down[0])
        back_buf = lax.all_to_all(expert_out, 'ep', 1, 1, tiled=True)
        pair_out = back_buf.reshape(-1, d_model)[pair_pos].reshape(n_tok, n_top, d_model)
        mixed_out = jnp.sum(pair_out.astype(jnp.float32) * topk_w[:, :, None], axis=1)
        return mixed_out.astype(jnp.bfloat16)

    row_spec = P(('dp', 'ep'), None)
    weight_spec = P('ep', None, None, None)
    return jax.shard_map(group_layer, mesh=mesh, in_specs=(row_spec, row_spec, row_spec, weight_spec, weight_spec, P(None, None)), out_specs=row_spec, check_vma=False)
```

profile of v0, /device:TPU:21, one launch (start us, length us, event | category | flops | bytes accessed | tf_op | source)
XLA Modules:
  0.0 574.5 jit_solution(17485200401106639298)
XLA Ops:
  0.0 0.8 copy.26
  0.8 0.1 eq.61
  0.9 0.1 eq.57
  1.0 0.1 reshape.255
  1.1 0.8 eq.53
  1.9 0.8 reshape.254
  2.7 0.1 copy.29
  2.8 0.2 fusion.31
  3.1 0.1 copy.30
  3.2 0.2 convert_reduce_fusion
  3.4 1.6 scatter_custom_fusion.1
  5.0 0.4 fusion.30
  5.4 6.6 %gather_fusion = s32[1024]{0:T(1024)S(1)} fusion(s32[128]{0:T(128)S(1)} %scatter_custom_fusion.1, s32[1024]{0:T(1024)S(1)} %broadcast_clamp_fusion.1), kind=kCustom, calls=%fused_computation | custom fusion | bytes 12288 | tf_op jit(solution)/shard_map/gather | solution.py:28
  11.9 0.4 fusion.41
  12.4 7.1 %scatter_fusion = s32[128,4]{0,1:T(4,128)S(1)} fusion(s32[128,4]{0,1:T(4,128)S(1)} %broadcast_in_dim.14, s32[144]{0:T(256)S(1)} %bitcast.41, s32[144]{0:T(256)S(1)} %iota.20), kind=kCustom, calls=%fused_computation.4 | custom fusion | bytes 2880 | tf_op jit(solution)/shard_map/scatter | solution.py:24
  19.5 8.7 %gather_fusion.1 = s32[1024]{0:T(1024)S(1)} fusion(s32[128,4]{0,1:T(4,128)S(1)} %scatter_fusion, s32[1024]{0:T(1024)S(1)} %bitcast.40), kind=kCustom, calls=%fused_computation.1 | custom fusion | bytes 16384 | tf_op jit(solution)/shard_map/gather | solution.py:29
  28.2 0.4 compare_select_fusion
  28.6 4.3 scatter_custom_fusion.2
  32.9 0.0 copy-done
  33.0 7.7 %gather_fusion.2 = bf16[1584,2048]{1,0:T(8,128)(2,1)} fusion(bf16[128,2048]{1,0:T(8,128)(2,1)S(1)} %copy-done, s32[2048]{0:T(1024)S(1)} %pad_clamp_fusion), kind=kCustom, calls=%fused_computation.2 | custom fusion | bytes 12982464 | tf_op jit(solution)/shard_map/gather | solution.py:50
  40.6 10.2 %reshape.257 = bf16[9,16,11,2048]{3,2,1,0:T(8,128)(2,1)} reshape(bf16[1584,2048]{1,0:T(8,128)(2,1)} %gather_fusion.2) | data formatting | bytes 12976128 | tf_op jit(solution)/shard_map/reshape | solution.py:50
  50.8 9.3 %copy.31 = bf16[9,16,11,2048]{3,2,0,1:T(8,128)(2,1)} copy(bf16[9,16,11,2048]{3,2,1,0:T(8,128)(2,1)} %reshape.257) | data formatting | bytes 12976128 | tf_op jit(solution)/shard_map/reshape | solution.py:50
  60.0 218.5 %all_to_all.10 = bf16[9,16,11,2048]{3,2,0,1:T(8,128)(2,1)} all-to-all(bf16[9,16,11,2048]{3,2,0,1:T(8,128)(2,1)} %copy.31), channel_id=1, replica_groups=mesh['dp'=4,'ep'=16] {'ep'}, dimensions={1} | all-to-all | bytes 12976128 | tf_op jit(solution)/shard_map/all_to_all | solution.py:51
  278.5 27.6 %fusion.14 = bf16[9,16,11,2048]{3,1,2,0:T(8,128)(2,1)} fusion(bf16[1,9,768,2048]{3,2,1,0:T(8,128)(2,1)} %param.10, bf16[1,9,2048,768]{3,2,1,0:T(8,128)(2,1)} %param.9, bf16[9,16,11,2048]{3,2,0,1:T(8,128)(2,1)} %all_to_all.10), kind=kOutput, calls=%fused_computation.23 | convolution fusion | flops 9979858944 | bytes 69599232 | tf_op jit(solution)/shard_map/spcf,sfm->spcm/dot_general | solution.py:40
  306.2 10.5 %copy.33 = bf16[9,16,11,2048]{3,2,0,1:T(8,128)(2,1)} copy(bf16[9,16,11,2048]{3,1,2,0:T(8,128)(2,1)} %fusion.14) | data formatting | bytes 12976128 | tf_op jit(solution)/shard_map/convert_element_type | solution.py:40
  316.6 5.2 all-to-all-start.1
  321.9 0.1 copy.35
  322.0 212.7 %all-to-all-done.1 = bf16[9,16,11,2048]{3,2,0,1:T(8,128)(2,1)} async-done(((bf16[9,16,11,2048]{3,2,0,1:T(8,128)(2,1)}), bf16[9,16,11,2048]{3,2,0,1:T(8,128)(2,1)}, u32[]{:S(2)}, u32[]{:S(2)}) %all-to-all-start.1) | async-done | bytes 6488096 | tf_op jit(solution)/shard_map/all_to_all | solution.py:53
  534.8 9.3 %copy.34 = bf16[9,16,11,2048]{3,2,1,0:T(8,128)(2,1)} copy(bf16[9,16,11,2048]{3,2,0,1:T(8,128)(2,1)} %all-to-all-done.1) | data formatting | bytes 12976128 | tf_op jit(solution)/shard_map/all_to_all | solution.py:53
  544.0 10.6 %reshape.258 = bf16[1584,2048]{1,0:T(8,128)(2,1)} reshape(bf16[9,16,11,2048]{3,2,1,0:T(8,128)(2,1)} %copy.34) | data formatting | bytes 12976128 | tf_op jit(solution)/shard_map/reshape | solution.py:54
  554.6 12.5 %gather_fusion.3 = bf16[1024,2048]{1,0:T(8,128)(2,1)} fusion(bf16[1584,2048]{1,0:T(8,128)(2,1)} %reshape.258, s32[1024]{0:T(1024)S(1)} %broadcast_clamp_fusion), kind=kCustom, calls=%fused_computation.3 | custom fusion | bytes 8392704 | tf_op jit(solution)/shard_map/gather | solution.py:54
  567.1 7.3 %fusion.4 = bf16[128,2048]{1,0:T(8,128)(2,1)} fusion(bf16[1024,2048]{1,0:T(8,128)(2,1)} %gather_fusion.3, f32[128,8]{1,0:T(8,128)S(1)} %copy.35), kind=kLoop, calls=%fused_computation.12 | loop fusion | flops 6029312 | bytes 4722688 | tf_op jit(solution)/shard_map/reduce_sum | solution.py:55
  (21 shorter events, 0.1 us)
Async XLA Ops:
  0.0 32.9 %copy-start = (bf16[128,2048]{1,0:T(8,128)(2,1)S(1)}, bf16[128,2048]{1,0:T(8,128)(2,1)}, u32[]{:S(2)}) copy-start(bf16[128,2048]{1,0:T(8,128)(2,1)} %param.6) | copy-start | bytes 1572868
  316.6 5.3 copy-start.2
  316.6 218.1 %all-to-all-start.1 = ((bf16[9,16,11,2048]{3,2,0,1:T(8,128)(2,1)}), bf16[9,16,11,2048]{3,2,0,1:T(8,128)(2,1)}, u32[]{:S(2)}, u32[]{:S(2)}) async-start(bf16[9,16,11,2048]{3,2,0,1:T(8,128)(2,1)} %copy.33), calls=%async_computation.1 | async-start | bytes 18874368 | tf_op jit(solution)/shard_map/all_to_all | solution.py:53
  554.6 19.9 %copy-start.1 = (bf16[128,2048]{1,0:T(8,128)(2,1)S(1)}, bf16[128,2048]{1,0:T(8,128)(2,1)}, u32[]{:S(2)}) copy-start(bf16[128,2048]{1,0:T(8,128)(2,1)} %param.6) | copy-start | bytes 1572868
where the time goes:
time: 575 us; the launch traced here: 574 us
  blocking collectives  218 us (38%)
  waiting for transfers between devices  213 us (37%)
  local copies, waits for them, and re-layouts  99.6 us (17%)
  matrix products  27.6 us (5%)
  other arithmetic  10.5 us (2%)
    all_to_all x1, blocking collectives, group_layer(): recv_buf = lax.all_to_all(send_buf, 'ep', 1, 1, tiled=True)  218 us
    all_to_all x1, waiting for transfers between devices, group_layer(): back_buf = lax.all_to_all(expert_out, 'ep', 1, 1, tiled=True)  213 us
    dot_general x1, matrix products, expert_ffn(): jnp.einsum('spcf,sfm->spcm', hidden, down_local, preferred_element_type=j...  27.6 us
    reshape x2, local copies, waits for them, and re-layouts, group_layer(): send_buf = tokens[buf_tok].reshape(n_slot, n_dev, capacity, d_model)  19.4 us
    gather x1, local copies, waits for them, and re-layouts, group_layer(): back_buf.reshape(-1, d_model)[pair_pos].reshape(n_tok, n_top, d_model)  12.5 us
  transfers between devices with their start and end apart: 1, of which 1 were waited for; matrix products, arithmetic and copies ran while one was open for 0% of the time, Pallas kernels for 0%

commit v1 on v0

v1 whole, which is shorter than its diff:
```python
import functools

import jax
import jax.numpy as jnp
from jax import lax
from jax.experimental import pallas as pl
from jax.experimental.pallas import tpu as pltpu
from jax.sharding import PartitionSpec as P

MESH = pl.DeviceIdType.MESH
F32 = jnp.float32
BF16 = jnp.bfloat16
CORES = 2
W_DEPTH = 3
AG_CHUNKS = 2
RS_CHUNKS = 4


def slot_bound(n_tok, n_top, n_dev, n_slot):
    base_load = (n_tok * n_top) // (n_dev * n_slot)
    return base_load + base_load // 2 + 1


def split3(x):
    hi = x.astype(BF16)
    rest = x - hi.astype(F32)
    mid = rest.astype(BF16)
    low = (rest - mid.astype(F32)).astype(BF16)
    return hi, mid, low


def layer_kernel(nz, tok_hbm, meta_hbm, slot_smem, slot_vmem, up_hbm, down_hbm, out_ref,
                 toks, metas, x_buf, o_sib, up_buf, down_buf, rs_buf, mix, pick, target,
                 in_sem, ag_send, ag_recv, sib_send, sib_recv, ms_send, ms_recv, mb_send, mb_recv,
                 w_sem, o_send, o_recv, rs_send, rs_recv):
    half = nz // 2
    n_tok, d_model = tok_hbm.shape
    n_top = meta_hbm.shape[0] // 2
    n_slot, cap = x_buf.shape[0], x_buf.shape[3]
    rows = n_slot * cap
    k_pad, n_exp = pick.shape
    ag_rows = n_tok // AG_CHUNKS
    rs_cols = d_model // RS_CHUNKS

    me = lax.axis_index("ep")
    z = me // CORES
    core = me % CORES
    other = 1 - core

    def ring(pos):
        return (pos + nz) % nz

    def device(pos, which):
        return {"ep": pos * CORES + which}

    def remote(src, dst, send, recv, dev):
        return pltpu.make_async_remote_copy(src_ref=src, dst_ref=dst, send_sem=send, recv_sem=recv,
                                            device_id=dev, device_id_type=MESH)

    def weight_copies(slot):
        buf = slot % W_DEPTH
        return (pltpu.make_async_copy(up_hbm.at[0, slot], up_buf.at[buf], w_sem.at[0, buf]),
                pltpu.make_async_copy(down_hbm.at[0, slot], down_buf.at[buf], w_sem.at[1, buf]))

    own_tok = pltpu.make_async_copy(tok_hbm, toks.at[core, z], in_sem.at[0])
    own_meta = pltpu.make_async_copy(meta_hbm, metas.at[core, z], in_sem.at[1])
    own_meta.start()
    own_tok.start()
    barrier = pltpu.get_barrier_semaphore()
    pl.semaphore_signal(barrier, inc=1, device_id=device(ring(z + 1), core), device_id_type=MESH)
    pl.semaphore_signal(barrier, inc=1, device_id=device(ring(z - 1), core), device_id_type=MESH)
    pl.semaphore_signal(barrier, inc=1, device_id=device(z, other), device_id_type=MESH)
    pl.semaphore_wait(barrier, 3)
    own_meta.wait()
    own_tok.wait()

    def ag_copy(d, hop, c):
        sign = 1 - 2 * d
        ref = toks.at[core, ring(z - sign * (hop - 1)), pl.ds(c * ag_rows, ag_rows)]
        return remote(ref, ref, ag_send.at[d, hop - 1, c], ag_recv.at[d, hop - 1, c], device(ring(z + sign), core))

    def ag_arrival(d, hop, c):
        sign = 1 - 2 * d
        ref = toks.at[core, ring(z - sign * hop), pl.ds(c * ag_rows, ag_rows)]
        return remote(ref, ref, ag_send.at[d, hop - 1, c], ag_recv.at[d, hop - 1, c], device(ring(z + sign), core))

    def sib_copy(d, hop, c, which):
        sign = 1 - 2 * d
        ref = toks.at[which, ring(z - sign * hop), pl.ds(c * ag_rows, ag_rows)]
        return remote(ref, ref, sib_send.at[d, hop, c], sib_recv.at[d, hop, c], device(z, other))

    def meta_copy(d, hop, back):
        sign = 1 - 2 * d
        ref = metas.at[core, ring(z - sign * (hop - 1 + back))]
        return remote(ref, ref, ms_send.at[d, hop - 1], ms_recv.at[d, hop - 1], device(ring(z + sign), core))

    def meta_sib(d, hop, which):
        sign = 1 - 2 * d
        ref = metas.at[which, ring(z - sign * hop)]
        return remote(ref, ref, mb_send.at[d, hop], mb_recv.at[d, hop], device(z, other))

    def chunk_order(d):
        return list(range(AG_CHUNKS)) if d == 0 else list(range(AG_CHUNKS))[::-1]

    def carried(d, hop):
        order = chunk_order(d)
        return order if hop < half else order[:AG_CHUNKS // 2]

    def meta_carried(d, hop):
        return hop < half or d == 0

    for d in range(2):
        meta_copy(d, 1, 0).start()
    for c in range(AG_CHUNKS):
        for d in range(2):
            ag_copy(d, 1, chunk_order(d)[c]).start()
    meta_sib(0, 0, core).start()
    for c in range(AG_CHUNKS):
        sib_copy(0, 0, c, core).start()
    for slot in range(W_DEPTH):
        for copy in weight_copies(slot):
            copy.start()

    lane = lax.broadcasted_iota(jnp.int32, (cap, n_exp), 1)
    row = lax.broadcasted_iota(jnp.int32, (cap, n_exp), 0).astype(F32)
    table = slot_vmem[...]
    place = lax.broadcasted_iota(jnp.int32, table.shape, 0) * n_slot + lax.broadcasted_iota(jnp.int32, table.shape, 1)
    for w in range(2):
        dev = me if w == 0 else z * CORES + other
        for s in range(n_slot):
            exp_id = slot_smem[dev, s]
            same = table == exp_id
            copies = jnp.sum(jnp.where(same, 1.0, 0.0))
            earlier = jnp.sum(jnp.where(same & (place < dev * n_slot + s), 1.0, 0.0))
            at = pl.ds(w * rows + s * cap, cap)
            pick[at, :] = jnp.where(lane == exp_id, 1.0, 0.0).astype(BF16)
            target[at, :] = row * copies + earlier
    if k_pad > 2 * rows:
        pick[2 * rows:, :] = jnp.zeros((k_pad - 2 * rows, n_exp), BF16)
        target[2 * rows:, :] = jnp.full((k_pad - 2 * rows, n_exp), -5.0, F32)

    def place_rows(which, pos, mine):
        info = metas[which, pos]
        exp_iota = lax.broadcasted_iota(jnp.int32, (n_exp, n_tok), 0).astype(F32)
        chosen = jnp.zeros((n_exp, n_tok), F32)
        gate = jnp.zeros((n_exp, n_tok), F32)
        for j in range(n_top):
            hit = exp_iota == info[j:j + 1, :]
            chosen = jnp.where(hit, 1.0, chosen)
            if mine:
                gate = jnp.where(hit, info[n_top + j:n_top + j + 1, :], gate)
        before = (lax.broadcasted_iota(jnp.int32, (n_tok, n_tok), 0)
                  < lax.broadcasted_iota(jnp.int32, (n_tok, n_tok), 1))
        rank = jnp.dot(chosen.astype(BF16), jnp.where(before, 1.0, 0.0).astype(BF16), preferred_element_type=F32)
        rank = jnp.where(chosen > 0.5, rank, -1.0).astype(BF16)
        n_rows = k_pad if mine else rows
        takes = jnp.dot(pick[:n_rows, :], rank, preferred_element_type=F32) == target[:n_rows, :]
        onehot = jnp.where(takes[:rows], 1.0, 0.0).astype(BF16)
        for c in range(RS_CHUNKS):
            cols = pl.ds(c * rs_cols, rs_cols)
            got = jnp.dot(onehot, toks[which, pos, :, cols], preferred_element_type=F32).astype(BF16)
            x_buf[:, which, pos, :, cols] = got.reshape(n_slot, cap, rs_cols)
        if mine:
            parts = [jnp.dot(pick[...], part, preferred_element_type=F32) for part in split3(gate)]
            picked = jnp.where(takes, parts[0] + parts[1] + parts[2], 0.0)
            for n, part in enumerate(split3(picked.T)):
                mix[pos, n * n_tok:(n + 1) * n_tok, :] = part

    place_rows(core, z, True)
    meta_sib(0, 0, other).wait_recv()
    for c in range(AG_CHUNKS):
        sib_copy(0, 0, c, other).wait_recv()
    place_rows(other, z, False)

    for hop in range(1, half + 1):
        for d in range(2):
            if meta_carried(d, hop):
                meta_copy(d, hop, 1).wait_recv()
                if hop < half and meta_carried(d, hop + 1):
                    meta_copy(d, hop + 1, 0).start()
                meta_sib(d, hop, core).start()
        for n in range(AG_CHUNKS):
            for d in range(2):
                if n < len(carried(d, hop)):
                    c = carried(d, hop)[n]
                    ag_arrival(d, hop, c).wait_recv()
                    if hop < half and c in carried(d, hop + 1):
                        ag_copy(d, hop + 1, c).start()
                    sib_copy(d, hop, c, core).start()
        n_dirs = 2 if hop < half else 1

        @pl.loop(0, n_dirs)
        def _(d):
            place_rows(core, ring(z - (1 - 2 * d) * hop), True)

        for d in range(2):
            if meta_carried(d, hop):
                meta_sib(d, hop, other).wait_recv()
            for c in carried(d, hop):
                sib_copy(d, hop, c, other).wait_recv()

        @pl.loop(0, n_dirs)
        def _(d):
            place_rows(other, ring(z - (1 - 2 * d) * hop), False)

    def o_copy(slot, which):
        return remote(x_buf.at[slot, which], o_sib.at[slot], o_send.at[slot], o_recv.at[slot], device(z, other))

    @pl.loop(0, n_slot)
    def _(slot):
        buf = slot % W_DEPTH
        for copy in weight_copies(slot):
            copy.wait()
        x = x_buf[slot].reshape(CORES * nz * cap, d_model)
        hidden = jax.nn.gelu(jnp.dot(x, up_buf[buf], preferred_element_type=F32), approximate=True).astype(BF16)
        for c in range(RS_CHUNKS):
            cols = pl.ds(c * rs_cols, rs_cols)
            o = jnp.dot(hidden, down_buf[buf, :, cols], preferred_element_type=F32).astype(BF16)
            x_buf[slot, :, :, :, cols] = o.reshape(CORES, nz, cap, rs_cols)
        o_copy(slot, other).start()

        @pl.when(slot + W_DEPTH < n_slot)
        def _():
            for copy in weight_copies(slot + W_DEPTH):
                copy.start()

    @pl.loop(0, n_slot)
    def _(slot):
        o_copy(slot, other).wait_recv()

    def own_sum(pos, c):
        cols = pl.ds(pl.multiple_of(c * rs_cols, rs_cols), rs_cols)
        parts = [x_buf[:, core, pos, :, cols].reshape(rows, rs_cols), o_sib[:, pos, :, cols].reshape(rows, rs_cols)]
        if k_pad > 2 * rows:
            parts.append(jnp.zeros((k_pad - 2 * rows, rs_cols), BF16))
        total = jnp.dot(mix[pos], jnp.concatenate(parts, axis=0), preferred_element_type=F32)
        return total[:n_tok] + total[n_tok:2 * n_tok] + total[2 * n_tok:]

    skip = RS_CHUNKS // 2
    items = half * RS_CHUNKS

    def rs_copy(d, n):
        sign = 1 - 2 * d
        return remote(rs_buf.at[d, n - skip], rs_buf.at[d, n - skip + RS_CHUNKS], rs_send.at[d, n],
                      rs_recv.at[d, n + RS_CHUNKS], device(ring(z + sign), core))

    def rs_arrival(d, n):
        sign = 1 - 2 * d
        return remote(rs_buf.at[d, n - skip], rs_buf.at[d, n - skip], rs_send.at[d, n], rs_recv.at[d, n],
                      device(ring(z + sign), core))

    def rs_chunk(d, n):
        c = n % RS_CHUNKS
        return (c + skip) % RS_CHUNKS if d == 0 else c

    @pl.loop(skip, items)
    def _(n):
        away = half - n // RS_CHUNKS
        for d in range(2):
            sign = 1 - 2 * d
            value = own_sum(ring(z + sign * away), rs_chunk(d, n))

            @pl.when(n < skip + RS_CHUNKS)
            def _():
                rs_buf[d, n - skip] = value

            @pl.when(n >= skip + RS_CHUNKS)
            def _():
                rs_arrival(d, n).wait_recv()
                rs_buf[d, n - skip] += value

            rs_copy(d, n).start()

    for c in range(RS_CHUNKS):
        value = own_sum(z, c)
        for d in range(2):
            n = items + ((c + skip) % RS_CHUNKS if d == 0 else c)
            rs_arrival(d, n).wait_recv()
            value += rs_buf[d, n - skip]
        out_ref[:, c * rs_cols:(c + 1) * rs_cols] = value.astype(BF16)

    for d in range(2):
        for hop in range(1, half + 1):
            if meta_carried(d, hop):
                meta_copy(d, hop, 0).wait_send()
                meta_sib(d, hop, core).wait_send()
            for c in carried(d, hop):
                ag_copy(d, hop, c).wait_send()
                sib_copy(d, hop, c, core).wait_send()
    meta_sib(0, 0, core).wait_send()
    for c in range(AG_CHUNKS):
        sib_copy(0, 0, c, core).wait_send()

    @pl.loop(0, n_slot)
    def _(slot):
        o_copy(slot, other).wait_send()

    @pl.loop(skip, items)
    def _(n):
        for d in range(2):
            rs_copy(d, n).wait_send()


def solution(mesh):
    n_dev = mesh.shape["ep"]
    nz = n_dev // CORES
    half = nz // 2

    def group_layer(tokens, topk_idx, topk_w, w_up, w_down, slot_expert):
        n_tok, d_model = tokens.shape
        n_top = topk_idx.shape[1]
        n_slot = slot_expert.shape[1]
        n_exp = n_dev * (n_slot - 1)
        d_ff = w_up.shape[3]
        cap = -(-slot_bound(n_tok, n_top, n_dev, n_slot) // 16) * 16
        k_pad = -(-2 * n_slot * cap // 128) * 128
        meta = jnp.concatenate([topk_idx.T.astype(F32), topk_w.T], axis=0)
        skip = RS_CHUNKS // 2
        dma = pltpu.SemaphoreType.DMA
        any_space = pl.BlockSpec(memory_space=pl.ANY)
        vmem = pl.BlockSpec(memory_space=pltpu.VMEM)
        return pl.pallas_call(
            functools.partial(layer_kernel, nz),
            out_shape=jax.ShapeDtypeStruct((n_tok, d_model), BF16),
            in_specs=[any_space, any_space, pl.BlockSpec(memory_space=pltpu.SMEM), vmem, any_space, any_space],
            out_specs=vmem,
            scratch_shapes=[
                pltpu.VMEM((CORES, nz, n_tok, d_model), BF16),
                pltpu.VMEM((CORES, nz, 2 * n_top, n_tok), F32),
                pltpu.VMEM((n_slot, CORES, nz, cap, d_model), BF16),
                pltpu.VMEM((n_slot, nz, cap, d_model), BF16),
                pltpu.VMEM((W_DEPTH, d_model, d_ff), BF16),
                pltpu.VMEM((W_DEPTH, d_ff, d_model), BF16),
                pltpu.VMEM((2, (half + 1) * RS_CHUNKS - skip, n_tok, d_model // RS_CHUNKS), F32),
                pltpu.VMEM((nz, 3 * n_tok, k_pad), BF16),
                pltpu.VMEM((k_pad, n_exp), BF16),
                pltpu.VMEM((k_pad, n_exp), F32),
                dma((2,)),
                dma((2, half, AG_CHUNKS)), dma((2, half, AG_CHUNKS)),
                dma((2, half + 1, AG_CHUNKS)), dma((2, half + 1, AG_CHUNKS)),
                dma((2, half)), dma((2, half)),
                dma((2, half + 1)), dma((2, half + 1)),
                dma((2, W_DEPTH)),
                dma((n_slot,)), dma((n_slot,)),
                dma((2, half * RS_CHUNKS)), dma((2, (half + 1) * RS_CHUNKS)),
            ],
            compiler_params=pltpu.CompilerParams(collective_id=0, has_side_effects=True,
                                                 vmem_limit_bytes=62 * 1024 * 1024),
        )(tokens, meta, slot_expert, slot_expert, w_up, w_down)

    row_spec = P(("dp", "ep"), None)
    weight_spec = P("ep", None, None, None)
    return jax.shard_map(group_layer, mesh=mesh,
                         in_specs=(row_spec, row_spec, row_spec, weight_spec, weight_spec, P(None, None)),
                         out_specs=row_spec, check_vma=False)
```

time: 575 us -> 163 us (0.28)
  blocking collectives: 218 us -> 0 us
  waiting for transfers between devices: 213 us -> 0 us
  Pallas kernels: 0 us -> 158 us
  local copies, waits for them, and re-layouts: 99.6 us -> 1.88 us
  matrix products: 27.6 us -> 0 us
  other arithmetic: 10.5 us -> 1.97 us
    all_to_all x1 -> x0, blocking collectives: 218 us -> none  [group_layer(): recv_buf = lax.all_to_all(send_buf, 'ep', 1, 1, tiled=True)]
    all_to_all x1 -> x0, waiting for transfers between devices: 213 us -> none  [group_layer(): back_buf = lax.all_to_all(expert_out, 'ep', 1, 1, tiled=True)]
    pallas_call x0 -> x1, Pallas kernels: none -> 158 us  [group_layer(): pl.pallas_call(functools.partial(layer_kernel, nz), out_shape=jax.ShapeDt...]
    gather x4 -> x0, local copies, waits for them, and re-layouts: 35.5 us -> none  [the longest x1 12.5 us: group_layer(): back_buf.reshape(-1, d_model)[pair_pos].reshape(n_tok, n_top, d_model)]
    reshape x5 -> x0, local copies, waits for them, and re-layouts: 30.9 us -> none  [the longest x2 19.4 us: group_layer(): send_buf = tokens[buf_tok].reshape(n_slot, n_dev, capacity, d_model)]
    dot_general x1 -> x0, matrix products: 27.6 us -> none  [expert_ffn(): jnp.einsum('spcf,sfm->spcm', hidden, down_local, preferred_element_type=j...]
    scatter x2 -> x0, local copies, waits for them, and re-layouts: 11.4 us -> none  [the longest x1 7.09 us: route_pairs(): jnp.zeros((n_exp, MAX_COPIES), jnp.int32).at[table_flat, copy_rank]]
    convert_element_type x1 -> x0, local copies, waits for them, and re-layouts: 10.5 us -> none  [expert_ffn(): jnp.einsum('spcf,sfm->spcm', hidden, down_local, preferred_element_type=j...]
  transfers between devices with their start and end apart: 1 -> 0, of which waited for: 1 -> 0; matrix products, arithmetic and copies ran while one was open for 0% -> 0% of each run, Pallas kernels for 0% -> 0%
where the time goes in v1:
time: 163 us; the launch traced here: 162 us
  Pallas kernels  158 us (97%)
  other arithmetic  1.97 us (1%)
  local copies, waits for them, and re-layouts  1.88 us (1%)
    pallas_call x1, Pallas kernels, group_layer(): pl.pallas_call(functools.partial(layer_kernel, nz), out_shape=jax.ShapeDt...  158 us

profile of v1, /device:TPU:21, one launch (start us, length us, event | category | flops | bytes accessed | tf_op | source)
XLA Modules:
  0.0 162.3 jit_solution(8929089928661037297)
XLA Ops:
  0.0 0.7 convert_bitcast_fusion
  0.7 1.3 pad_maximum_fusion.meta_hbm
  2.0 158.4 %shard_map.64 = bf16[128,2048]{1,0:T(8,128)(2,1)} custom-call(bf16[128,2048]{1,0:T(8,128)(2,1)} %tok_hbm.1, f32[16,128]{1,0:T(8,128)} %pad_maximum_fusion.meta_hbm, s32[16,9]{1,0:T(8,128)} %slot_vmem.1, s32[16,9]{1,0:T(8,128)} %slot_vmem.1, bf16[1,9,2048,768]{3,2,1,0:T(8,128)(2,1)} %up_hbm.1, bf16[1,9,768,2048]{3,2,1,0:T(8,128)(2,1)} %down_hbm.1), custom_call_target="tpu_custom_call" | custom-call | tf_op jit(solution)/shard_map/pallas_call | solution.py:322
  160.4 1.9 %copy.8 = bf16[128,2048]{1,0:T(8,128)(2,1)} copy(bf16[128,2048]{1,0:T(8,128)(2,1)} %shard_map.64) | data formatting | bytes 1048576

commit v2 on v1

--- a/solution.py
+++ b/solution.py
@@ -14,6 +14,8 @@
 W_DEPTH = 3
 AG_CHUNKS = 2
 RS_CHUNKS = 4
+AG2_HOP = 3
+AG2_STEPS = ((1, 1, 0), (3, 1, 1), (4, 2, 0), (5, 2, 1), (7, 3, 0), (8, 3, 1))
 
 
 def slot_bound(n_tok, n_top, n_dev, n_slot):
@@ -57,8 +59,8 @@
         return pltpu.make_async_remote_copy(src_ref=src, dst_ref=dst, send_sem=send, recv_sem=recv,
                                             device_id=dev, device_id_type=MESH)
 
-    def weight_copies(slot):
-        buf = slot % W_DEPTH
+    def weight_copies(step):
+        buf, slot = step % W_DEPTH, step % n_slot
         return (pltpu.make_async_copy(up_hbm.at[0, slot], up_buf.at[buf], w_sem.at[0, buf]),
                 pltpu.make_async_copy(down_hbm.at[0, slot], down_buf.at[buf], w_sem.at[1, buf]))
 
@@ -111,14 +113,18 @@
 
     for d in range(2):
         meta_copy(d, 1, 0).start()
-    for c in range(AG_CHUNKS):
-        for d in range(2):
-            ag_copy(d, 1, chunk_order(d)[c]).start()
     meta_sib(0, 0, core).start()
-    for c in range(AG_CHUNKS):
-        sib_copy(0, 0, c, core).start()
-    for slot in range(W_DEPTH):
-        for copy in weight_copies(slot):
+
+    @pl.when(core == 0)
+    def _():
+        for c in range(AG_CHUNKS):
+            for d in range(2):
+                ag_copy(d, 1, chunk_order(d)[c]).start()
+        for c in range(AG_CHUNKS):
+            sib_copy(0, 0, c, core).start()
+
+    for step in range(W_DEPTH):
+        for copy in weight_copies(step):
             copy.start()
 
     lane = lax.broadcasted_iota(jnp.int32, (cap, n_exp), 1)
@@ -139,94 +145,128 @@
         pick[2 * rows:, :] = jnp.zeros((k_pad - 2 * rows, n_exp), BF16)
         target[2 * rows:, :] = jnp.full((k_pad - 2 * rows, n_exp), -5.0, F32)
 
-    def place_rows(which, pos, mine):
+    def place_rows(which, pos):
         info = metas[which, pos]
         exp_iota = lax.broadcasted_iota(jnp.int32, (n_exp, n_tok), 0).astype(F32)
         chosen = jnp.zeros((n_exp, n_tok), F32)
-        gate = jnp.zeros((n_exp, n_tok), F32)
         for j in range(n_top):
-            hit = exp_iota == info[j:j + 1, :]
-            chosen = jnp.where(hit, 1.0, chosen)
-            if mine:
-                gate = jnp.where(hit, info[n_top + j:n_top + j + 1, :], gate)
+            chosen = jnp.where(exp_iota == info[j:j + 1, :], 1.0, chosen)
         before = (lax.broadcasted_iota(jnp.int32, (n_tok, n_tok), 0)
                   < lax.broadcasted_iota(jnp.int32, (n_tok, n_tok), 1))
         rank = jnp.dot(chosen.astype(BF16), jnp.where(before, 1.0, 0.0).astype(BF16), preferred_element_type=F32)
         rank = jnp.where(chosen > 0.5, rank, -1.0).astype(BF16)
-        n_rows = k_pad if mine else rows
-        takes = jnp.dot(pick[:n_rows, :], rank, preferred_element_type=F32) == target[:n_rows, :]
-        onehot = jnp.where(takes[:rows], 1.0, 0.0).astype(BF16)
+        takes = jnp.dot(pick[:rows, :], rank, preferred_element_type=F32) == target[:rows, :]
+        onehot = jnp.where(takes, 1.0, 0.0).astype(BF16)
         for c in range(RS_CHUNKS):
             cols = pl.ds(c * rs_cols, rs_cols)
             got = jnp.dot(onehot, toks[which, pos, :, cols], preferred_element_type=F32).astype(BF16)
             x_buf[:, which, pos, :, cols] = got.reshape(n_slot, cap, rs_cols)
-        if mine:
+
+        @pl.when(core == which)
+        def _():
+            gate = jnp.zeros((n_exp, n_tok), F32)
+            for j in range(n_top):
+                gate = jnp.where(exp_iota == info[j:j + 1, :], info[n_top + j:n_top + j + 1, :], gate)
+            takes = jnp.dot(pick[...], rank, preferred_element_type=F32) == target[...]
             parts = [jnp.dot(pick[...], part, preferred_element_type=F32) for part in split3(gate)]
             picked = jnp.where(takes, parts[0] + parts[1] + parts[2], 0.0)
             for n, part in enumerate(split3(picked.T)):
                 mix[pos, n * n_tok:(n + 1) * n_tok, :] = part
 
-    place_rows(core, z, True)
-    meta_sib(0, 0, other).wait_recv()
-    for c in range(AG_CHUNKS):
-        sib_copy(0, 0, c, other).wait_recv()
-    place_rows(other, z, False)
-
-    for hop in range(1, half + 1):
+    def start_gather():
+        for c in range(AG_CHUNKS):
+            for d in range(2):
+                ag_copy(d, 1, chunk_order(d)[c]).start()
+        for c in range(AG_CHUNKS):
+            sib_copy(0, 0, c, core).start()
+
+    def pass_on(hop, n):
         for d in range(2):
-            if meta_carried(d, hop):
-                meta_copy(d, hop, 1).wait_recv()
-                if hop < half and meta_carried(d, hop + 1):
-                    meta_copy(d, hop + 1, 0).start()
-                meta_sib(d, hop, core).start()
-        for n in range(AG_CHUNKS):
-            for d in range(2):
-                if n < len(carried(d, hop)):
-                    c = carried(d, hop)[n]
-                    ag_arrival(d, hop, c).wait_recv()
-                    if hop < half and c in carried(d, hop + 1):
-                        ag_copy(d, hop + 1, c).start()
-                    sib_copy(d, hop, c, core).start()
-        n_dirs = 2 if hop < half else 1
-
-        @pl.loop(0, n_dirs)
-        def _(d):
-            place_rows(core, ring(z - (1 - 2 * d) * hop), True)
-
+            if n < len(carried(d, hop)):
+                c = carried(d, hop)[n]
+                ag_arrival(d, hop, c).wait_recv()
+                if hop < half and c in carried(d, hop + 1):
+                    ag_copy(d, hop + 1, c).start()
+                sib_copy(d, hop, c, core).start()
+
+    def from_sibling(hop):
+        if hop == 0:
+            for c in range(AG_CHUNKS):
+                sib_copy(0, 0, c, other).wait_recv()
+            return
         for d in range(2):
-            if meta_carried(d, hop):
-                meta_sib(d, hop, other).wait_recv()
             for c in carried(d, hop):
                 sib_copy(d, hop, c, other).wait_recv()
 
-        @pl.loop(0, n_dirs)
+    def place_hop(which, hop):
+        @pl.loop(0, 1 if hop in (0, half) else 2)
         def _(d):
-            place_rows(other, ring(z - (1 - 2 * d) * hop), False)
-
-    def o_copy(slot, which):
-        return remote(x_buf.at[slot, which], o_sib.at[slot], o_send.at[slot], o_recv.at[slot], device(z, other))
-
-    @pl.loop(0, n_slot)
-    def _(slot):
-        buf = slot % W_DEPTH
-        for copy in weight_copies(slot):
+            place_rows(which, ring(z - (1 - 2 * d) * hop))
+
+    meta_sib(0, 0, other).wait_recv()
+    for hop in range(half + 1):
+        if hop > 0:
+            for d in range(2):
+                if meta_carried(d, hop):
+                    meta_copy(d, hop, 1).wait_recv()
+                    if hop < half and meta_carried(d, hop + 1):
+                        meta_copy(d, hop + 1, 0).start()
+                    meta_sib(d, hop, core).start()
+
+        @pl.when(core == 0)
+        def _():
+            if hop > 0:
+                for n in range(len(carried(0, hop))):
+                    pass_on(hop, n)
+
+        @pl.when(core == 1)
+        def _():
+            from_sibling(hop)
+            if hop == AG2_HOP:
+                start_gather()
+
+        if hop > 0:
+            for d in range(2):
+                if meta_carried(d, hop):
+                    meta_sib(d, hop, other).wait_recv()
+        place_hop(0, hop)
+
+    def o_copy(slot):
+        return remote(x_buf.at[slot, other], o_sib.at[slot], o_send.at[slot], o_recv.at[slot], device(z, other))
+
+    def experts(slot, batch):
+        step = batch * n_slot + slot
+        buf = step % W_DEPTH
+        for copy in weight_copies(step):
             copy.wait()
-        x = x_buf[slot].reshape(CORES * nz * cap, d_model)
+        x = x_buf[slot, batch].reshape(nz * cap, d_model)
         hidden = jax.nn.gelu(jnp.dot(x, up_buf[buf], preferred_element_type=F32), approximate=True).astype(BF16)
         for c in range(RS_CHUNKS):
             cols = pl.ds(c * rs_cols, rs_cols)
             o = jnp.dot(hidden, down_buf[buf, :, cols], preferred_element_type=F32).astype(BF16)
-            x_buf[slot, :, :, :, cols] = o.reshape(CORES, nz, cap, rs_cols)
-        o_copy(slot, other).start()
-
-        @pl.when(slot + W_DEPTH < n_slot)
-        def _():
-            for copy in weight_copies(slot + W_DEPTH):
+            x_buf[slot, batch, :, :, cols] = o.reshape(nz, cap, rs_cols)
+
+        @pl.when(core != batch)
+        def _():
+            o_copy(slot).start()
+
+        @pl.when(step + W_DEPTH < 2 * n_slot)
+        def _():
+            for copy in weight_copies(step + W_DEPTH):
                 copy.start()
 
     @pl.loop(0, n_slot)
     def _(slot):
-        o_copy(slot, other).wait_recv()
+        experts(slot, 0)
+        for after, hop, n in AG2_STEPS:
+            @pl.when((core == 1) & (slot == after))
+            def _():
+                pass_on(hop, n)
+
+    def from_sibling_o():
+        @pl.loop(0, n_slot)
+        def _(slot):
+            o_copy(slot).wait_recv()
 
     def own_sum(pos, c):
         cols = pl.ds(pl.multiple_of(c * rs_cols, rs_cols), rs_cols)
@@ -253,8 +293,7 @@
         c = n % RS_CHUNKS
         return (c + skip) % RS_CHUNKS if d == 0 else c
 
-    @pl.loop(skip, items)
-    def _(n):
+    def rs_item(n):
         away = half - n // RS_CHUNKS
         for d in range(2):
             sign = 1 - 2 * d
@@ -270,6 +309,37 @@
                 rs_buf[d, n - skip] += value
 
             rs_copy(d, n).start()
+
+    @pl.when(core == 0)
+    def _():
+        from_sibling_o()
+        pl.loop(skip, skip + RS_CHUNKS)(rs_item)
+
+    @pl.when(core == 1)
+    def _():
+        for n in range(len(carried(0, half))):
+            pass_on(half, n)
+
+    for hop in range(half + 1):
+        @pl.when(core == 0)
+        def _():
+            from_sibling(hop)
+
+        place_hop(1, hop)
+
+    @pl.loop(0, n_slot)
+    def _(slot):
+        experts(slot, 1)
+
+        @pl.when(core == 0)
+        def _():
+            rs_item(skip + RS_CHUNKS + slot)
+
+    @pl.when(core == 1)
+    def _():
+        from_sibling_o()
+
+    pl.loop(jnp.where(core == 0, skip + RS_CHUNKS + n_slot, skip), items)(rs_item)
 
     for c in range(RS_CHUNKS):
         value = own_sum(z, c)
@@ -293,7 +363,7 @@
 
     @pl.loop(0, n_slot)
     def _(slot):
-        o_copy(slot, other).wait_send()
+        o_copy(slot).wait_send()
 
     @pl.loop(skip, items)
     def _(n):

time: 163 us -> 140 us (0.86)
  Pallas kernels: 158 us -> 136 us
    pallas_call x1, Pallas kernels: 158 us -> 136 us  [group_layer(): pl.pallas_call(functools.partial(layer_kernel, nz), out_shape=jax.ShapeDt...]
where the time goes in v2:
time: 140 us
  Pallas kernels  136 us (97%)
  other arithmetic  1.97 us (1%)
  local copies, waits for them, and re-layouts  1.88 us (1%)
    pallas_call x1, Pallas kernels, group_layer(): pl.pallas_call(functools.partial(layer_kernel, nz), out_shape=jax.ShapeDt...  136 us

profile of v2, /device:TPU:21, one launch (start us, length us, event | category | flops | bytes accessed | tf_op | source)
XLA Modules:
  0.0 140.1 jit_solution(11916989649173683959)
XLA Ops:
  0.0 0.7 convert_bitcast_fusion
  0.7 1.3 pad_maximum_fusion.meta_hbm
  2.0 136.3 %shard_map.64 = bf16[128,2048]{1,0:T(8,128)(2,1)} custom-call(bf16[128,2048]{1,0:T(8,128)(2,1)} %tok_hbm.1, f32[16,128]{1,0:T(8,128)} %pad_maximum_fusion.meta_hbm, s32[16,9]{1,0:T(8,128)} %slot_vmem.1, s32[16,9]{1,0:T(8,128)} %slot_vmem.1, bf16[1,9,2048,768]{3,2,1,0:T(8,128)(2,1)} %up_hbm.1, bf16[1,9,768,2048]{3,2,1,0:T(8,128)(2,1)} %down_hbm.1), custom_call_target="tpu_custom_call" | custom-call | tf_op jit(solution)/shard_map/pallas_call | solution.py:392
  138.2 1.9 %copy.8 = bf16[128,2048]{1,0:T(8,128)(2,1)} copy(bf16[128,2048]{1,0:T(8,128)(2,1)} %shard_map.64) | data formatting | bytes 1048576

commit v3 on v2

--- a/solution.py
+++ b/solution.py
@@ -15,12 +15,16 @@
 AG_CHUNKS = 2
 RS_CHUNKS = 4
 AG2_HOP = 3
-AG2_STEPS = ((1, 1, 0), (3, 1, 1), (4, 2, 0), (5, 2, 1), (7, 3, 0), (8, 3, 1))
+AG2_STEPS = ((0, 1, 0), (2, 1, 1), (3, 2, 0), (5, 2, 1), (7, 3, 0), (8, 3, 1))
 
 
 def slot_bound(n_tok, n_top, n_dev, n_slot):
     base_load = (n_tok * n_top) // (n_dev * n_slot)
     return base_load + base_load // 2 + 1
+
+
+def round_up(n, unit):
+    return -(-n // unit) * unit
 
 
 def split3(x):
@@ -31,16 +35,18 @@
     return hi, mid, low
 
 
-def layer_kernel(nz, tok_hbm, meta_hbm, slot_smem, slot_vmem, up_hbm, down_hbm, out_ref,
-                 toks, metas, x_buf, o_sib, up_buf, down_buf, rs_buf, mix, pick, target,
+def layer_kernel(nz, bound, tok_hbm, idx_hbm, gate_hbm, slot_smem, slot_vmem, up_hbm, down_hbm, out_ref,
+                 toks, idx_own, metas, x_buf, o_sib, up_buf, down_buf, rs_buf, first_out, first_in, total_buf,
+                 mix, mix_up, pick, target, pick_up, target_up, pack,
                  in_sem, ag_send, ag_recv, sib_send, sib_recv, ms_send, ms_recv, mb_send, mb_recv,
                  w_sem, o_send, o_recv, rs_send, rs_recv):
     half = nz // 2
     n_tok, d_model = tok_hbm.shape
-    n_top = meta_hbm.shape[0] // 2
+    n_top = idx_hbm.shape[0]
     n_slot, cap = x_buf.shape[0], x_buf.shape[3]
     rows = n_slot * cap
     k_pad, n_exp = pick.shape
+    packed, packed_pad = first_out.shape[2], pack.shape[0]
     ag_rows = n_tok // AG_CHUNKS
     rs_cols = d_model // RS_CHUNKS
 
@@ -65,16 +71,20 @@
                 pltpu.make_async_copy(down_hbm.at[0, slot], down_buf.at[buf], w_sem.at[1, buf]))
 
     own_tok = pltpu.make_async_copy(tok_hbm, toks.at[core, z], in_sem.at[0])
-    own_meta = pltpu.make_async_copy(meta_hbm, metas.at[core, z], in_sem.at[1])
-    own_meta.start()
+    own_idx = pltpu.make_async_copy(idx_hbm, idx_own, in_sem.at[1])
+    own_gate = pltpu.make_async_copy(gate_hbm, metas.at[core, z, n_top:], in_sem.at[2])
     own_tok.start()
+    own_idx.start()
+    own_gate.start()
     barrier = pltpu.get_barrier_semaphore()
     pl.semaphore_signal(barrier, inc=1, device_id=device(ring(z + 1), core), device_id_type=MESH)
     pl.semaphore_signal(barrier, inc=1, device_id=device(ring(z - 1), core), device_id_type=MESH)
     pl.semaphore_signal(barrier, inc=1, device_id=device(z, other), device_id_type=MESH)
+    own_idx.wait()
+    metas[core, z, :n_top, :] = idx_own[...].astype(F32)
+    own_gate.wait()
+    own_tok.wait()
     pl.semaphore_wait(barrier, 3)
-    own_meta.wait()
-    own_tok.wait()
 
     def ag_copy(d, hop, c):
         sign = 1 - 2 * d
@@ -110,10 +120,6 @@
 
     def meta_carried(d, hop):
         return hop < half or d == 0
-
-    for d in range(2):
-        meta_copy(d, 1, 0).start()
-    meta_sib(0, 0, core).start()
 
     @pl.when(core == 0)
     def _():
@@ -123,6 +129,9 @@
         for c in range(AG_CHUNKS):
             sib_copy(0, 0, c, core).start()
 
+    for d in range(2):
+        meta_copy(d, 1, 0).start()
+    meta_sib(0, 0, core).start()
     for step in range(W_DEPTH):
         for copy in weight_copies(step):
             copy.start()
@@ -131,30 +140,66 @@
     row = lax.broadcasted_iota(jnp.int32, (cap, n_exp), 0).astype(F32)
     table = slot_vmem[...]
     place = lax.broadcasted_iota(jnp.int32, table.shape, 0) * n_slot + lax.broadcasted_iota(jnp.int32, table.shape, 1)
-    for w in range(2):
-        dev = me if w == 0 else z * CORES + other
-        for s in range(n_slot):
-            exp_id = slot_smem[dev, s]
-            same = table == exp_id
-            copies = jnp.sum(jnp.where(same, 1.0, 0.0))
-            earlier = jnp.sum(jnp.where(same & (place < dev * n_slot + s), 1.0, 0.0))
-            at = pl.ds(w * rows + s * cap, cap)
-            pick[at, :] = jnp.where(lane == exp_id, 1.0, 0.0).astype(BF16)
-            target[at, :] = row * copies + earlier
     if k_pad > 2 * rows:
         pick[2 * rows:, :] = jnp.zeros((k_pad - 2 * rows, n_exp), BF16)
-        target[2 * rows:, :] = jnp.full((k_pad - 2 * rows, n_exp), -5.0, F32)
-
-    def place_rows(which, pos):
-        info = metas[which, pos]
-        exp_iota = lax.broadcasted_iota(jnp.int32, (n_exp, n_tok), 0).astype(F32)
+        target[2 * rows:, :] = jnp.full((k_pad - 2 * rows, n_exp), -1.0, F32)
+
+    def slot_rows(pos):
+        for w in range(2):
+            dev = pos * CORES + (core if w == 0 else other)
+            for s in range(n_slot):
+                exp_id = slot_smem[dev, s]
+                same = table == exp_id
+                copies = jnp.sum(jnp.where(same, 1.0, 0.0))
+                earlier = jnp.sum(jnp.where(same & (place < dev * n_slot + s), 1.0, 0.0))
+                at = pl.ds(w * rows + s * cap, cap)
+                pick[at, :] = jnp.where(lane == exp_id, 1.0, 0.0).astype(BF16)
+                target[at, :] = row * copies + earlier
+
+    column = lax.broadcasted_iota(jnp.int32, (packed_pad, k_pad), 1)
+    side = jnp.where(column >= rows, 1, 0)
+    in_side = column - side * rows
+    in_slot = in_side % cap
+    packed_row = side * (packed // 2) + (in_side // cap) * bound + in_slot
+    used = (in_slot < bound) & (column < 2 * rows)
+    pack[...] = jnp.where(used & (lax.broadcasted_iota(jnp.int32, (packed_pad, k_pad), 0) == packed_row),
+                          1.0, 0.0).astype(BF16)
+    for d in range(2):
+        slot_rows(ring(z - (1 - 2 * d)))
+        pick_up[d] = jnp.dot(pack[...], pick[...], preferred_element_type=F32).astype(BF16)
+        target_up[d] = jnp.dot(pack[...], (target[...] + 1.0).astype(BF16), preferred_element_type=F32) - 1.0
+    slot_rows(z)
+
+    exp_iota = lax.broadcasted_iota(jnp.int32, (n_exp, n_tok), 0).astype(F32)
+
+    def ranks(info):
         chosen = jnp.zeros((n_exp, n_tok), F32)
         for j in range(n_top):
             chosen = jnp.where(exp_iota == info[j:j + 1, :], 1.0, chosen)
         before = (lax.broadcasted_iota(jnp.int32, (n_tok, n_tok), 0)
                   < lax.broadcasted_iota(jnp.int32, (n_tok, n_tok), 1))
         rank = jnp.dot(chosen.astype(BF16), jnp.where(before, 1.0, 0.0).astype(BF16), preferred_element_type=F32)
-        rank = jnp.where(chosen > 0.5, rank, -1.0).astype(BF16)
+        return jnp.where(chosen > 0.5, rank, -1.0).astype(BF16)
+
+    def mixing(info, rank, picks, targets):
+        gate = jnp.zeros((n_exp, n_tok), F32)
+        for j in range(n_top):
+            gate = jnp.where(exp_iota == info[j:j + 1, :], info[n_top + j:n_top + j + 1, :], gate)
+        takes = jnp.dot(picks, rank, preferred_element_type=F32) == targets
+        parts = [jnp.dot(picks, part, preferred_element_type=F32) for part in split3(gate)]
+        return split3(jnp.where(takes, parts[0] + parts[1] + parts[2], 0.0).T)
+
+    def mix_first_hop():
+        @pl.loop(0, 4)
+        def _(i):
+            d, j = i // 2, i % 2
+            info = metas[core, ring(z + (1 - 2 * d) * (half - 1 - j))]
+            for n, part in enumerate(mixing(info, ranks(info), pick_up[d], target_up[d])):
+                mix_up[d, j, n * n_tok:(n + 1) * n_tok, :] = part
+
+    def place_rows(which, pos):
+        info = metas[which, pos]
+        rank = ranks(info)
         takes = jnp.dot(pick[:rows, :], rank, preferred_element_type=F32) == target[:rows, :]
         onehot = jnp.where(takes, 1.0, 0.0).astype(BF16)
         for c in range(RS_CHUNKS):
@@ -164,13 +209,7 @@
 
         @pl.when(core == which)
         def _():
-            gate = jnp.zeros((n_exp, n_tok), F32)
-            for j in range(n_top):
-                gate = jnp.where(exp_iota == info[j:j + 1, :], info[n_top + j:n_top + j + 1, :], gate)
-            takes = jnp.dot(pick[...], rank, preferred_element_type=F32) == target[...]
-            parts = [jnp.dot(pick[...], part, preferred_element_type=F32) for part in split3(gate)]
-            picked = jnp.where(takes, parts[0] + parts[1] + parts[2], 0.0)
-            for n, part in enumerate(split3(picked.T)):
+            for n, part in enumerate(mixing(info, rank, pick[...], target[...])):
                 mix[pos, n * n_tok:(n + 1) * n_tok, :] = part
 
     def start_gather():
@@ -230,6 +269,10 @@
                 if meta_carried(d, hop):
                     meta_sib(d, hop, other).wait_recv()
         place_hop(0, hop)
+        if hop == half - 1:
+            @pl.when(core == 0)
+            def _():
+                mix_first_hop()
 
     def o_copy(slot):
         return remote(x_buf.at[slot, other], o_sib.at[slot], o_send.at[slot], o_recv.at[slot], device(z, other))
@@ -268,52 +311,77 @@
         def _(slot):
             o_copy(slot).wait_recv()
 
-    def own_sum(pos, c):
+    def chip_rows(pos, c):
         cols = pl.ds(pl.multiple_of(c * rs_cols, rs_cols), rs_cols)
         parts = [x_buf[:, core, pos, :, cols].reshape(rows, rs_cols), o_sib[:, pos, :, cols].reshape(rows, rs_cols)]
         if k_pad > 2 * rows:
             parts.append(jnp.zeros((k_pad - 2 * rows, rs_cols), BF16))
-        total = jnp.dot(mix[pos], jnp.concatenate(parts, axis=0), preferred_element_type=F32)
+        return jnp.concatenate(parts, axis=0)
+
+    def mixed(weights, values):
+        total = jnp.dot(weights, values, preferred_element_type=F32)
         return total[:n_tok] + total[n_tok:2 * n_tok] + total[2 * n_tok:]
 
+    def own_sum(pos, c):
+        return mixed(mix[pos], chip_rows(pos, c))
+
     skip = RS_CHUNKS // 2
+    first = skip + RS_CHUNKS
     items = half * RS_CHUNKS
-
-    def rs_copy(d, n):
-        sign = 1 - 2 * d
-        return remote(rs_buf.at[d, n - skip], rs_buf.at[d, n - skip + RS_CHUNKS], rs_send.at[d, n],
-                      rs_recv.at[d, n + RS_CHUNKS], device(ring(z + sign), core))
-
-    def rs_arrival(d, n):
-        sign = 1 - 2 * d
-        return remote(rs_buf.at[d, n - skip], rs_buf.at[d, n - skip], rs_send.at[d, n], rs_recv.at[d, n],
-                      device(ring(z + sign), core))
 
     def rs_chunk(d, n):
         c = n % RS_CHUNKS
         return (c + skip) % RS_CHUNKS if d == 0 else c
 
-    def rs_item(n):
-        away = half - n // RS_CHUNKS
-        for d in range(2):
-            sign = 1 - 2 * d
-            value = own_sum(ring(z + sign * away), rs_chunk(d, n))
-
-            @pl.when(n < skip + RS_CHUNKS)
-            def _():
-                rs_buf[d, n - skip] = value
-
-            @pl.when(n >= skip + RS_CHUNKS)
-            def _():
-                rs_arrival(d, n).wait_recv()
-                rs_buf[d, n - skip] += value
-
+    def rs_dest(d, n):
+        return ring(z + (1 - 2 * d) * (half - n // RS_CHUNKS))
+
+    def first_copy(d, n):
+        return remote(first_out.at[d, n - skip], first_in.at[d, n - skip], rs_send.at[d, n],
+                      rs_recv.at[d, n + RS_CHUNKS], device(ring(z + (1 - 2 * d)), core))
+
+    def first_arrival(d, n):
+        return remote(first_out.at[d, n - first], first_in.at[d, n - first], rs_send.at[d, n],
+                      rs_recv.at[d, n], device(ring(z + (1 - 2 * d)), core))
+
+    def rs_copy(d, n):
+        return remote(rs_buf.at[d, n - first], rs_buf.at[d, n - first + RS_CHUNKS], rs_send.at[d, n],
+                      rs_recv.at[d, n + RS_CHUNKS], device(ring(z + (1 - 2 * d)), core))
+
+    def rs_arrival(d, n):
+        return remote(rs_buf.at[d, n - first], rs_buf.at[d, n - first], rs_send.at[d, n], rs_recv.at[d, n],
+                      device(ring(z + (1 - 2 * d)), core))
+
+    def first_item(n):
+        for d in range(2):
+            got = jnp.dot(pack[:packed, :], chip_rows(rs_dest(d, n), rs_chunk(d, n)), preferred_element_type=F32)
+            first_out[d, n - skip] = got.astype(BF16)
+            first_copy(d, n).start()
+
+    def second_item(n):
+        for d in range(2):
+            value = own_sum(rs_dest(d, n), rs_chunk(d, n))
+            first_arrival(d, n).wait_recv()
+            rows_in = first_in[d, n - first]
+            if packed_pad > packed:
+                rows_in = jnp.concatenate([rows_in, jnp.zeros((packed_pad - packed, rs_cols), BF16)], axis=0)
+            rs_buf[d, n - first] = value + mixed(mix_up[d, (n - first) // skip], rows_in)
             rs_copy(d, n).start()
+
+    def later_item(n):
+        for d in range(2):
+            value = own_sum(rs_dest(d, n), rs_chunk(d, n))
+            rs_arrival(d, n).wait_recv()
+            rs_buf[d, n - first] += value
+            rs_copy(d, n).start()
+
+    def start_chains():
+        from_sibling_o()
+        pl.loop(skip, first)(first_item)
 
     @pl.when(core == 0)
     def _():
-        from_sibling_o()
-        pl.loop(skip, skip + RS_CHUNKS)(rs_item)
+        start_chains()
 
     @pl.when(core == 1)
     def _():
@@ -331,23 +399,33 @@
     def _(slot):
         experts(slot, 1)
 
-        @pl.when(core == 0)
-        def _():
-            rs_item(skip + RS_CHUNKS + slot)
+        @pl.when((core == 0) & (slot < RS_CHUNKS))
+        def _():
+            second_item(first + slot)
+
+        @pl.when((core == 0) & (slot >= RS_CHUNKS))
+        def _():
+            later_item(first + slot)
 
     @pl.when(core == 1)
     def _():
-        from_sibling_o()
-
-    pl.loop(jnp.where(core == 0, skip + RS_CHUNKS + n_slot, skip), items)(rs_item)
+        mix_first_hop()
+        start_chains()
+        pl.loop(first, first + RS_CHUNKS)(second_item)
+
+    pl.loop(jnp.where(core == 0, first + n_slot, first + RS_CHUNKS), items)(later_item)
 
     for c in range(RS_CHUNKS):
-        value = own_sum(z, c)
-        for d in range(2):
-            n = items + ((c + skip) % RS_CHUNKS if d == 0 else c)
-            rs_arrival(d, n).wait_recv()
-            value += rs_buf[d, n - skip]
-        out_ref[:, c * rs_cols:(c + 1) * rs_cols] = value.astype(BF16)
+        total_buf[c] = own_sum(z, c)
+    for i in range(RS_CHUNKS):
+        for d in range(2):
+            rs_arrival(d, items + i).wait_recv()
+        if i >= skip:
+            for c in (i - skip, i):
+                value = total_buf[c]
+                for d in range(2):
+                    value += rs_buf[d, items - first + ((c + skip) % RS_CHUNKS if d == 0 else c)]
+                out_ref[:, c * rs_cols:(c + 1) * rs_cols] = value.astype(BF16)
 
     for d in range(2):
         for hop in range(1, half + 1):
@@ -365,7 +443,12 @@
     def _(slot):
         o_copy(slot).wait_send()
 
-    @pl.loop(skip, items)
+    @pl.loop(skip, first)
+    def _(n):
+        for d in range(2):
+            first_copy(d, n).wait_send()
+
+    @pl.loop(first, items)
     def _(n):
         for d in range(2):
             rs_copy(d, n).wait_send()
@@ -382,30 +465,41 @@
         n_slot = slot_expert.shape[1]
         n_exp = n_dev * (n_slot - 1)
         d_ff = w_up.shape[3]
-        cap = -(-slot_bound(n_tok, n_top, n_dev, n_slot) // 16) * 16
-        k_pad = -(-2 * n_slot * cap // 128) * 128
-        meta = jnp.concatenate([topk_idx.T.astype(F32), topk_w.T], axis=0)
+        bound = slot_bound(n_tok, n_top, n_dev, n_slot)
+        cap = round_up(bound, 16)
+        k_pad = round_up(2 * n_slot * cap, 128)
+        packed = 2 * round_up(n_slot * bound, 8)
+        packed_pad = round_up(packed, 128)
+        rs_cols = d_model // RS_CHUNKS
         skip = RS_CHUNKS // 2
         dma = pltpu.SemaphoreType.DMA
         any_space = pl.BlockSpec(memory_space=pl.ANY)
         vmem = pl.BlockSpec(memory_space=pltpu.VMEM)
         return pl.pallas_call(
-            functools.partial(layer_kernel, nz),
+            functools.partial(layer_kernel, nz, bound),
             out_shape=jax.ShapeDtypeStruct((n_tok, d_model), BF16),
-            in_specs=[any_space, any_space, pl.BlockSpec(memory_space=pltpu.SMEM), vmem, any_space, any_space],
+            in_specs=[any_space, any_space, any_space, pl.BlockSpec(memory_space=pltpu.SMEM), vmem, any_space, any_space],
             out_specs=vmem,
             scratch_shapes=[
                 pltpu.VMEM((CORES, nz, n_tok, d_model), BF16),
+                pltpu.VMEM((n_top, n_tok), jnp.int32),
                 pltpu.VMEM((CORES, nz, 2 * n_top, n_tok), F32),
                 pltpu.VMEM((n_slot, CORES, nz, cap, d_model), BF16),
                 pltpu.VMEM((n_slot, nz, cap, d_model), BF16),
                 pltpu.VMEM((W_DEPTH, d_model, d_ff), BF16),
                 pltpu.VMEM((W_DEPTH, d_ff, d_model), BF16),
-                pltpu.VMEM((2, (half + 1) * RS_CHUNKS - skip, n_tok, d_model // RS_CHUNKS), F32),
+                pltpu.VMEM((2, half * RS_CHUNKS - skip, n_tok, rs_cols), F32),
+                pltpu.VMEM((2, RS_CHUNKS, packed, rs_cols), BF16),
+                pltpu.VMEM((2, RS_CHUNKS, packed, rs_cols), BF16),
+                pltpu.VMEM((RS_CHUNKS, n_tok, rs_cols), F32),
                 pltpu.VMEM((nz, 3 * n_tok, k_pad), BF16),
+                pltpu.VMEM((2, 2, 3 * n_tok, packed_pad), BF16),
                 pltpu.VMEM((k_pad, n_exp), BF16),
                 pltpu.VMEM((k_pad, n_exp), F32),
-                dma((2,)),
+                pltpu.VMEM((2, packed_pad, n_exp), BF16),
+                pltpu.VMEM((2, packed_pad, n_exp), F32),
+                pltpu.VMEM((packed_pad, k_pad), BF16),
+                dma((3,)),
                 dma((2, half, AG_CHUNKS)), dma((2, half, AG_CHUNKS)),
                 dma((2, half + 1, AG_CHUNKS)), dma((2, half + 1, AG_CHUNKS)),
                 dma((2, half)), dma((2, half)),
@@ -416,7 +510,7 @@
             ],
             compiler_params=pltpu.CompilerParams(collective_id=0, has_side_effects=True,
                                                  vmem_limit_bytes=62 * 1024 * 1024),
-        )(tokens, meta, slot_expert, slot_expert, w_up, w_down)
+        )(tokens, topk_idx.T, topk_w.T, slot_expert, slot_expert, w_up, w_down)
 
     row_spec = P(("dp", "ep"), None)
     weight_spec = P("ep", None, None, None)

time: 140 us -> 138 us (0.986)
  other arithmetic: 1.97 us -> 0 us
where the time goes in v3:
time: 138 us
  Pallas kernels  136 us (99%)
  local copies, waits for them, and re-layouts  1.88 us (1%)
    pallas_call x1, Pallas kernels, group_layer(): pl.pallas_call(functools.partial(layer_kernel, nz, bound), out_shape=jax....  136 us

profile of v3, /device:TPU:21, one launch (start us, length us, event | category | flops | bytes accessed | tf_op | source)
XLA Modules:
  0.0 137.7 jit_solution(17112580385510501311)
XLA Ops:
  0.0 135.8 %shard_map.64 = bf16[128,2048]{1,0:T(8,128)(2,1)} custom-call(bf16[128,2048]{1,0:T(8,128)(2,1)} %tok_hbm.1, s32[8,128]{1,0:T(8,128)} %bitcast.2, f32[8,128]{1,0:T(8,128)} %bitcast.3, s32[16,9]{1,0:T(8,128)} %slot_vmem.1, s32[16,9]{1,0:T(8,128)} %slot_vmem.1, bf16[1,9,2048,768]{3,2,1,0:T(8,128)(2,1)} %up_hbm.1, bf16[1,9,768,2048]{3,2,1,0:T(8,128)(2,1)} %down_hbm.1), custom_call_target="tpu_custom_call" | custom-call | tf_op jit(solution)/shard_map/pallas_call | solution.py:478
  135.8 1.9 %copy.8 = bf16[128,2048]{1,0:T(8,128)(2,1)} copy(bf16[128,2048]{1,0:T(8,128)(2,1)} %shard_map.64) | data formatting | bytes 1048576

commit v4 on v3

--- a/solution.py
+++ b/solution.py
@@ -121,6 +121,10 @@
     def meta_carried(d, hop):
         return hop < half or d == 0
 
+    for d in range(2):
+        meta_copy(d, 1, 0).start()
+    meta_sib(0, 0, core).start()
+
     @pl.when(core == 0)
     def _():
         for c in range(AG_CHUNKS):
@@ -129,9 +133,6 @@
         for c in range(AG_CHUNKS):
             sib_copy(0, 0, c, core).start()
 
-    for d in range(2):
-        meta_copy(d, 1, 0).start()
-    meta_sib(0, 0, core).start()
     for step in range(W_DEPTH):
         for copy in weight_copies(step):
             copy.start()
@@ -242,7 +243,11 @@
         def _(d):
             place_rows(which, ring(z - (1 - 2 * d) * hop))
 
-    meta_sib(0, 0, other).wait_recv()
+    def meta_from_sibling(hop):
+        for d in range(2):
+            if (hop == 0 and d == 0) or (hop > 0 and meta_carried(d, hop)):
+                meta_sib(d, hop, other).wait_recv()
+
     for hop in range(half + 1):
         if hop > 0:
             for d in range(2):
@@ -260,14 +265,11 @@
 
         @pl.when(core == 1)
         def _():
+            meta_from_sibling(hop)
             from_sibling(hop)
             if hop == AG2_HOP:
                 start_gather()
 
-        if hop > 0:
-            for d in range(2):
-                if meta_carried(d, hop):
-                    meta_sib(d, hop, other).wait_recv()
         place_hop(0, hop)
         if hop == half - 1:
             @pl.when(core == 0)
@@ -391,6 +393,7 @@
     for hop in range(half + 1):
         @pl.when(core == 0)
         def _():
+            meta_from_sibling(hop)
             from_sibling(hop)
 
         place_hop(1, hop)

time: 138 us -> 135 us (0.978)
  Pallas kernels: 136 us -> 132 us
    pallas_call x1, Pallas kernels: 136 us -> 132 us  [group_layer(): pl.pallas_call(functools.partial(layer_kernel, nz, bound), out_shape=jax....]
where the time goes in v4:
time: 135 us; the launch traced here: 134 us
  Pallas kernels  132 us (98%)
  local copies, waits for them, and re-layouts  1.88 us (1%)
    pallas_call x1, Pallas kernels, group_layer(): pl.pallas_call(functools.partial(layer_kernel, nz, bound), out_shape=jax....  132 us

profile of v4, /device:TPU:21, one launch (start us, length us, event | category | flops | bytes accessed | tf_op | source)
XLA Modules:
  0.0 134.4 jit_solution(1059759619803822638)
XLA Ops:
  0.0 132.5 %shard_map.64 = bf16[128,2048]{1,0:T(8,128)(2,1)} custom-call(bf16[128,2048]{1,0:T(8,128)(2,1)} %tok_hbm.1, s32[8,128]{1,0:T(8,128)} %bitcast.2, f32[8,128]{1,0:T(8,128)} %bitcast.3, s32[16,9]{1,0:T(8,128)} %slot_vmem.1, s32[16,9]{1,0:T(8,128)} %slot_vmem.1, bf16[1,9,2048,768]{3,2,1,0:T(8,128)(2,1)} %up_hbm.1, bf16[1,9,768,2048]{3,2,1,0:T(8,128)(2,1)} %down_hbm.1), custom_call_target="tpu_custom_call" | custom-call | tf_op jit(solution)/shard_map/pallas_call | solution.py:481
  132.5 1.9 %copy.8 = bf16[128,2048]{1,0:T(8,128)(2,1)} copy(bf16[128,2048]{1,0:T(8,128)(2,1)} %shard_map.64) | data formatting | bytes 1048576

commit v5 on v4

--- a/solution.py
+++ b/solution.py
@@ -11,11 +11,11 @@
 F32 = jnp.float32
 BF16 = jnp.bfloat16
 CORES = 2
-W_DEPTH = 3
-AG_CHUNKS = 2
+W_DEPTH = 4
+AG_CHUNKS = 4
 RS_CHUNKS = 4
+AG2_LATE = (((3, 0), (3, 1)), ((3, 2), (3, 3)), ((4, 0), (4, 1)), (), ())
 AG2_HOP = 3
-AG2_STEPS = ((0, 1, 0), (2, 1, 1), (3, 2, 0), (5, 2, 1), (7, 3, 0), (8, 3, 1))
 
 
 def slot_bound(n_tok, n_top, n_dev, n_slot):
@@ -35,8 +35,8 @@
     return hi, mid, low
 
 
-def layer_kernel(nz, bound, tok_hbm, idx_hbm, gate_hbm, slot_smem, slot_vmem, up_hbm, down_hbm, out_ref,
-                 toks, idx_own, metas, x_buf, o_sib, up_buf, down_buf, rs_buf, first_out, first_in, total_buf,
+def layer_kernel(nz, bound, tok_hbm, idx_hbm, gate_hbm, slot_hbm, up_hbm, down_hbm, out_ref,
+                 toks, idx_own, slot_smem, slot_vmem, metas, x_buf, o_sib, up_buf, down_buf, rs_buf, first_out, first_in, total_buf,
                  mix, mix_up, pick, target, pick_up, target_up, pack,
                  in_sem, ag_send, ag_recv, sib_send, sib_recv, ms_send, ms_recv, mb_send, mb_recv,
                  w_sem, o_send, o_recv, rs_send, rs_recv):
@@ -73,9 +73,12 @@
     own_tok = pltpu.make_async_copy(tok_hbm, toks.at[core, z], in_sem.at[0])
     own_idx = pltpu.make_async_copy(idx_hbm, idx_own, in_sem.at[1])
     own_gate = pltpu.make_async_copy(gate_hbm, metas.at[core, z, n_top:], in_sem.at[2])
+    tables = [pltpu.make_async_copy(slot_hbm, ref, in_sem.at[3 + n]) for n, ref in enumerate((slot_smem, slot_vmem))]
     own_tok.start()
     own_idx.start()
     own_gate.start()
+    for copy in tables:
+        copy.start()
     barrier = pltpu.get_barrier_semaphore()
     pl.semaphore_signal(barrier, inc=1, device_id=device(ring(z + 1), core), device_id_type=MESH)
     pl.semaphore_signal(barrier, inc=1, device_id=device(ring(z - 1), core), device_id_type=MESH)
@@ -139,6 +142,8 @@
 
     lane = lax.broadcasted_iota(jnp.int32, (cap, n_exp), 1)
     row = lax.broadcasted_iota(jnp.int32, (cap, n_exp), 0).astype(F32)
+    for copy in tables:
+        copy.wait()
     table = slot_vmem[...]
     place = lax.broadcasted_iota(jnp.int32, table.shape, 0) * n_slot + lax.broadcasted_iota(jnp.int32, table.shape, 1)
     if k_pad > 2 * rows:
@@ -303,10 +308,15 @@
     @pl.loop(0, n_slot)
     def _(slot):
         experts(slot, 0)
-        for after, hop, n in AG2_STEPS:
-            @pl.when((core == 1) & (slot == after))
-            def _():
-                pass_on(hop, n)
+
+        @pl.when((core == 1) & (slot < 2 * AG_CHUNKS))
+        def _():
+            hop, n = 1 + slot // AG_CHUNKS, slot % AG_CHUNKS
+            for d in range(2):
+                c = n if d == 0 else AG_CHUNKS - 1 - n
+                ag_arrival(d, hop, c).wait_recv()
+                ag_copy(d, hop + 1, c).start()
+                sib_copy(d, hop, c, core).start()
 
     def from_sibling_o():
         @pl.loop(0, n_slot)
@@ -385,16 +395,16 @@
     def _():
         start_chains()
 
-    @pl.when(core == 1)
-    def _():
-        for n in range(len(carried(0, half))):
-            pass_on(half, n)
-
     for hop in range(half + 1):
         @pl.when(core == 0)
         def _():
             meta_from_sibling(hop)
             from_sibling(hop)
+
+        @pl.when(core == 1)
+        def _():
+            for late, n in AG2_LATE[hop]:
+                pass_on(late, n)
 
         place_hop(1, hop)
 
@@ -481,11 +491,13 @@
         return pl.pallas_call(
             functools.partial(layer_kernel, nz, bound),
             out_shape=jax.ShapeDtypeStruct((n_tok, d_model), BF16),
-            in_specs=[any_space, any_space, any_space, pl.BlockSpec(memory_space=pltpu.SMEM), vmem, any_space, any_space],
+            in_specs=[any_space] * 6,
             out_specs=vmem,
             scratch_shapes=[
                 pltpu.VMEM((CORES, nz, n_tok, d_model), BF16),
                 pltpu.VMEM((n_top, n_tok), jnp.int32),
+                pltpu.SMEM(slot_expert.shape, jnp.int32),
+                pltpu.VMEM(slot_expert.shape, jnp.int32),
                 pltpu.VMEM((CORES, nz, 2 * n_top, n_tok), F32),
                 pltpu.VMEM((n_slot, CORES, nz, cap, d_model), BF16),
                 pltpu.VMEM((n_slot, nz, cap, d_model), BF16),
@@ -502,7 +514,7 @@
                 pltpu.VMEM((2, packed_pad, n_exp), BF16),
                 pltpu.VMEM((2, packed_pad, n_exp), F32),
                 pltpu.VMEM((packed_pad, k_pad), BF16),
-                dma((3,)),
+                dma((5,)),
                 dma((2, half, AG_CHUNKS)), dma((2, half, AG_CHUNKS)),
                 dma((2, half + 1, AG_CHUNKS)), dma((2, half + 1, AG_CHUNKS)),
                 dma((2, half)), dma((2, half)),
@@ -512,8 +524,8 @@
                 dma((2, half * RS_CHUNKS)), dma((2, (half + 1) * RS_CHUNKS)),
             ],
             compiler_params=pltpu.CompilerParams(collective_id=0, has_side_effects=True,
-                                                 vmem_limit_bytes=62 * 1024 * 1024),
-        )(tokens, topk_idx.T, topk_w.T, slot_expert, slot_expert, w_up, w_down)
+                                                 vmem_limit_bytes=67043328),
+        )(tokens, topk_idx.T, topk_w.T, slot_expert, w_up, w_down)
 
     row_spec = P(("dp", "ep"), None)
     weight_spec = P("ep", None, None, None)

time: 135 us -> 133 us (0.985)
    pallas_call x1, Pallas kernels: 132 us -> 131 us  [group_layer(): pl.pallas_call(functools.partial(layer_kernel, nz, bound), out_shape=jax....]
where the time goes in v5:
time: 133 us
  Pallas kernels  131 us (98%)
  local copies, waits for them, and re-layouts  1.88 us (1%)
    pallas_call x1, Pallas kernels, group_layer(): pl.pallas_call(functools.partial(layer_kernel, nz, bound), out_shape=jax....  131 us

profile of v5, /device:TPU:21, one launch (start us, length us, event | category | flops | bytes accessed | tf_op | source)
XLA Modules:
  0.0 132.9 jit_solution(6546882919298869340)
XLA Ops:
  0.0 131.0 %shard_map.64 = bf16[128,2048]{1,0:T(8,128)(2,1)} custom-call(bf16[128,2048]{1,0:T(8,128)(2,1)} %tok_hbm.1, s32[8,128]{1,0:T(8,128)} %bitcast.2, f32[8,128]{1,0:T(8,128)} %bitcast.3, s32[16,9]{1,0:T(8,128)} %slot_hbm.1, bf16[1,9,2048,768]{3,2,1,0:T(8,128)(2,1)} %up_hbm.1, bf16[1,9,768,2048]{3,2,1,0:T(8,128)(2,1)} %down_hbm.1), custom_call_target="tpu_custom_call" | custom-call | tf_op jit(solution)/shard_map/pallas_call | solution.py:491
  131.1 1.9 %copy.8 = bf16[128,2048]{1,0:T(8,128)(2,1)} copy(bf16[128,2048]{1,0:T(8,128)(2,1)} %shard_map.64) | data formatting | bytes 1048576

commit v6 on v5

--- a/solution.py
+++ b/solution.py
@@ -407,26 +407,25 @@
                 pass_on(late, n)
 
         place_hop(1, hop)
+        if hop > 0:
+            @pl.when(core == 0)
+            def _():
+                second_item(first + hop - 1)
 
     @pl.loop(0, n_slot)
     def _(slot):
         experts(slot, 1)
 
-        @pl.when((core == 0) & (slot < RS_CHUNKS))
-        def _():
-            second_item(first + slot)
-
-        @pl.when((core == 0) & (slot >= RS_CHUNKS))
-        def _():
-            later_item(first + slot)
+        @pl.when((core == 0) & (slot < items - first - RS_CHUNKS))
+        def _():
+            later_item(first + RS_CHUNKS + slot)
 
     @pl.when(core == 1)
     def _():
         mix_first_hop()
         start_chains()
         pl.loop(first, first + RS_CHUNKS)(second_item)
-
-    pl.loop(jnp.where(core == 0, first + n_slot, first + RS_CHUNKS), items)(later_item)
+        pl.loop(first + RS_CHUNKS, items)(later_item)
 
     for c in range(RS_CHUNKS):
         total_buf[c] = own_sum(z, c)

time: 133 us -> 133 us (level)
  no operation moved by 1% of the time
where the time goes in v6:
time: 133 us
  Pallas kernels  131 us (98%)
  local copies, waits for them, and re-layouts  1.88 us (1%)
    pallas_call x1, Pallas kernels, group_layer(): pl.pallas_call(functools.partial(layer_kernel, nz, bound), out_shape=jax....  131 us

profile of v6, /device:TPU:21, one launch (start us, length us, event | category | flops | bytes accessed | tf_op | source)
XLA Modules:
  0.0 132.9 jit_solution(12744879126614098680)
XLA Ops:
  0.0 131.0 %shard_map.64 = bf16[128,2048]{1,0:T(8,128)(2,1)} custom-call(bf16[128,2048]{1,0:T(8,128)(2,1)} %tok_hbm.1, s32[8,128]{1,0:T(8,128)} %bitcast.2, f32[8,128]{1,0:T(8,128)} %bitcast.3, s32[16,9]{1,0:T(8,128)} %slot_hbm.1, bf16[1,9,2048,768]{3,2,1,0:T(8,128)(2,1)} %up_hbm.1, bf16[1,9,768,2048]{3,2,1,0:T(8,128)(2,1)} %down_hbm.1), custom_call_target="tpu_custom_call" | custom-call | tf_op jit(solution)/shard_map/pallas_call | solution.py:490
  131.1 1.9 %copy.8 = bf16[128,2048]{1,0:T(8,128)(2,1)} copy(bf16[128,2048]{1,0:T(8,128)(2,1)} %shard_map.64) | data formatting | bytes 1048576

commit v7 on v6

--- a/solution.py
+++ b/solution.py
@@ -39,14 +39,14 @@
                  toks, idx_own, slot_smem, slot_vmem, metas, x_buf, o_sib, up_buf, down_buf, rs_buf, first_out, first_in, total_buf,
                  mix, mix_up, pick, target, pick_up, target_up, pack,
                  in_sem, ag_send, ag_recv, sib_send, sib_recv, ms_send, ms_recv, mb_send, mb_recv,
-                 w_sem, o_send, o_recv, rs_send, rs_recv):
+                 w_sem, o_send, o_recv, first_send, first_recv, rs_send, rs_recv):
     half = nz // 2
     n_tok, d_model = tok_hbm.shape
     n_top = idx_hbm.shape[0]
     n_slot, cap = x_buf.shape[0], x_buf.shape[3]
     rows = n_slot * cap
     k_pad, n_exp = pick.shape
-    packed, packed_pad = first_out.shape[2], pack.shape[0]
+    packed, packed_pad = first_out.shape[3], pack.shape[0]
     ag_rows = n_tok // AG_CHUNKS
     rs_cols = d_model // RS_CHUNKS
 
@@ -83,11 +83,13 @@
     pl.semaphore_signal(barrier, inc=1, device_id=device(ring(z + 1), core), device_id_type=MESH)
     pl.semaphore_signal(barrier, inc=1, device_id=device(ring(z - 1), core), device_id_type=MESH)
     pl.semaphore_signal(barrier, inc=1, device_id=device(z, other), device_id_type=MESH)
+    pl.semaphore_signal(barrier, inc=1, device_id=device(ring(z + 1), other), device_id_type=MESH)
+    pl.semaphore_signal(barrier, inc=1, device_id=device(ring(z - 1), other), device_id_type=MESH)
     own_idx.wait()
     metas[core, z, :n_top, :] = idx_own[...].astype(F32)
     own_gate.wait()
     own_tok.wait()
-    pl.semaphore_wait(barrier, 3)
+    pl.semaphore_wait(barrier, 5)
 
     def ag_copy(d, hop, c):
         sign = 1 - 2 * d
@@ -348,13 +350,14 @@
     def rs_dest(d, n):
         return ring(z + (1 - 2 * d) * (half - n // RS_CHUNKS))
 
-    def first_copy(d, n):
-        return remote(first_out.at[d, n - skip], first_in.at[d, n - skip], rs_send.at[d, n],
-                      rs_recv.at[d, n + RS_CHUNKS], device(ring(z + (1 - 2 * d)), core))
-
-    def first_arrival(d, n):
-        return remote(first_out.at[d, n - first], first_in.at[d, n - first], rs_send.at[d, n],
-                      rs_recv.at[d, n], device(ring(z + (1 - 2 * d)), core))
+    def first_copy(batch, d, j):
+        side = jnp.where(core == batch, 0, 1)
+        return remote(first_out.at[batch, d, j], first_in.at[side, d, j], first_send.at[batch, d, j],
+                      first_recv.at[side, d, j], device(ring(z + (1 - 2 * d)), batch))
+
+    def first_arrival(side, d, j):
+        return remote(first_out.at[0, d, j], first_in.at[side, d, j], first_send.at[0, d, j],
+                      first_recv.at[side, d, j], device(ring(z + (1 - 2 * d)), core))
 
     def rs_copy(d, n):
         return remote(rs_buf.at[d, n - first], rs_buf.at[d, n - first + RS_CHUNKS], rs_send.at[d, n],
@@ -364,21 +367,34 @@
         return remote(rs_buf.at[d, n - first], rs_buf.at[d, n - first], rs_send.at[d, n], rs_recv.at[d, n],
                       device(ring(z + (1 - 2 * d)), core))
 
-    def first_item(n):
-        for d in range(2):
-            got = jnp.dot(pack[:packed, :], chip_rows(rs_dest(d, n), rs_chunk(d, n)), preferred_element_type=F32)
-            first_out[d, n - skip] = got.astype(BF16)
-            first_copy(d, n).start()
-
-    def second_item(n):
-        for d in range(2):
-            value = own_sum(rs_dest(d, n), rs_chunk(d, n))
-            first_arrival(d, n).wait_recv()
-            rows_in = first_in[d, n - first]
-            if packed_pad > packed:
-                rows_in = jnp.concatenate([rows_in, jnp.zeros((packed_pad - packed, rs_cols), BF16)], axis=0)
-            rs_buf[d, n - first] = value + mixed(mix_up[d, (n - first) // skip], rows_in)
-            rs_copy(d, n).start()
+    def start_chains(batch):
+        k_own = round_up(rows, 128)
+        for j in range(2):
+            for d in range(2):
+                got = []
+                for n in (skip + 2 * j, skip + 2 * j + 1):
+                    cols = pl.ds(rs_chunk(d, n) * rs_cols, rs_cols)
+                    parts = [x_buf[:, batch, rs_dest(d, n), :, cols].reshape(rows, rs_cols)]
+                    if k_own > rows:
+                        parts.append(jnp.zeros((k_own - rows, rs_cols), BF16))
+                    got.append(jnp.dot(pack[:round_up(packed // 2, 16), :k_own], jnp.concatenate(parts, axis=0),
+                                       preferred_element_type=F32)[:packed // 2])
+                first_out[batch, d, j] = jnp.concatenate(got, axis=0).astype(BF16)
+                first_copy(batch, d, j).start()
+
+    def second_pair(j):
+        for d in range(2):
+            for side in range(2):
+                first_arrival(side, d, j).wait_recv()
+            sides = [first_in[side, d, j].astype(F32) for side in range(2)]
+            for i in range(2):
+                n = first + 2 * j + i
+                parts = [part[i * (packed // 2):(i + 1) * (packed // 2)] for part in sides]
+                if packed_pad > packed:
+                    parts.append(jnp.zeros((packed_pad - packed, rs_cols), F32))
+                rows_in = jnp.concatenate(parts, axis=0).astype(BF16)
+                rs_buf[d, n - first] = own_sum(rs_dest(d, n), rs_chunk(d, n)) + mixed(mix_up[d, j], rows_in)
+                rs_copy(d, n).start()
 
     def later_item(n):
         for d in range(2):
@@ -387,13 +403,11 @@
             rs_buf[d, n - first] += value
             rs_copy(d, n).start()
 
-    def start_chains():
-        from_sibling_o()
-        pl.loop(skip, first)(first_item)
+    start_chains(0)
 
     @pl.when(core == 0)
     def _():
-        start_chains()
+        from_sibling_o()
 
     for hop in range(half + 1):
         @pl.when(core == 0)
@@ -407,10 +421,10 @@
                 pass_on(late, n)
 
         place_hop(1, hop)
-        if hop > 0:
+        if hop in (1, 2):
             @pl.when(core == 0)
             def _():
-                second_item(first + hop - 1)
+                second_pair(hop - 1)
 
     @pl.loop(0, n_slot)
     def _(slot):
@@ -420,11 +434,14 @@
         def _():
             later_item(first + RS_CHUNKS + slot)
 
+    start_chains(1)
+
     @pl.when(core == 1)
     def _():
         mix_first_hop()
-        start_chains()
-        pl.loop(first, first + RS_CHUNKS)(second_item)
+        from_sibling_o()
+        for j in range(2):
+            second_pair(j)
         pl.loop(first + RS_CHUNKS, items)(later_item)
 
     for c in range(RS_CHUNKS):
@@ -455,10 +472,10 @@
     def _(slot):
         o_copy(slot).wait_send()
 
-    @pl.loop(skip, first)
-    def _(n):
-        for d in range(2):
-            first_copy(d, n).wait_send()
+    for batch in range(2):
+        for d in range(2):
+            for j in range(2):
+                first_copy(batch, d, j).wait_send()
 
     @pl.loop(first, items)
     def _(n):
@@ -503,8 +520,8 @@
                 pltpu.VMEM((W_DEPTH, d_model, d_ff), BF16),
                 pltpu.VMEM((W_DEPTH, d_ff, d_model), BF16),
                 pltpu.VMEM((2, half * RS_CHUNKS - skip, n_tok, rs_cols), F32),
-                pltpu.VMEM((2, RS_CHUNKS, packed, rs_cols), BF16),
-                pltpu.VMEM((2, RS_CHUNKS, packed, rs_cols), BF16),
+                pltpu.VMEM((2, 2, 2, packed, rs_cols), BF16),
+                pltpu.VMEM((2, 2, 2, packed, rs_cols), BF16),
                 pltpu.VMEM((RS_CHUNKS, n_tok, rs_cols), F32),
                 pltpu.VMEM((nz, 3 * n_tok, k_pad), BF16),
                 pltpu.VMEM((2, 2, 3 * n_tok, packed_pad), BF16),
@@ -520,6 +537,7 @@
                 dma((2, half + 1)), dma((2, half + 1)),
                 dma((2, W_DEPTH)),
                 dma((n_slot,)), dma((n_slot,)),
+                dma((2, 2, 2)), dma((2, 2, 2)),
                 dma((2, half * RS_CHUNKS)), dma((2, (half + 1) * RS_CHUNKS)),
             ],
             compiler_params=pltpu.CompilerParams(collective_id=0, has_side_effects=True,

time: 133 us -> 133 us (level)
  no operation moved by 1% of the time
where the time goes in v7:
time: 133 us
  Pallas kernels  131 us (98%)
  local copies, waits for them, and re-layouts  1.88 us (1%)
    pallas_call x1, Pallas kernels, group_layer(): pl.pallas_call(functools.partial(layer_kernel, nz, bound), out_shape=jax....  131 us

profile of v7, /device:TPU:21, one launch (start us, length us, event | category | flops | bytes accessed | tf_op | source)
XLA Modules:
  0.0 132.9 jit_solution(8422620066657432832)
XLA Ops:
  0.0 131.0 %shard_map.64 = bf16[128,2048]{1,0:T(8,128)(2,1)} custom-call(bf16[128,2048]{1,0:T(8,128)(2,1)} %tok_hbm.1, s32[8,128]{1,0:T(8,128)} %bitcast.2, f32[8,128]{1,0:T(8,128)} %bitcast.3, s32[16,9]{1,0:T(8,128)} %slot_hbm.1, bf16[1,9,2048,768]{3,2,1,0:T(8,128)(2,1)} %up_hbm.1, bf16[1,9,768,2048]{3,2,1,0:T(8,128)(2,1)} %down_hbm.1), custom_call_target="tpu_custom_call" | custom-call | tf_op jit(solution)/shard_map/pallas_call | solution.py:507
  131.0 1.9 %copy.8 = bf16[128,2048]{1,0:T(8,128)(2,1)} copy(bf16[128,2048]{1,0:T(8,128)(2,1)} %shard_map.64) | data formatting | bytes 1048576

commit v8 on v7

--- a/solution.py
+++ b/solution.py
@@ -430,10 +430,6 @@
     def _(slot):
         experts(slot, 1)
 
-        @pl.when((core == 0) & (slot < items - first - RS_CHUNKS))
-        def _():
-            later_item(first + RS_CHUNKS + slot)
-
     start_chains(1)
 
     @pl.when(core == 1)
@@ -442,7 +438,8 @@
         from_sibling_o()
         for j in range(2):
             second_pair(j)
-        pl.loop(first + RS_CHUNKS, items)(later_item)
+
+    pl.loop(first + RS_CHUNKS, items)(later_item)
 
     for c in range(RS_CHUNKS):
         total_buf[c] = own_sum(z, c)

time: 133 us -> 141 us (1.060)
  Pallas kernels: 131 us -> 139 us
    pallas_call x1, Pallas kernels: 131 us -> 139 us  [group_layer(): pl.pallas_call(functools.partial(layer_kernel, nz, bound), out_shape=jax....]
where the time goes in v8:
time: 141 us
  Pallas kernels  139 us (99%)
  local copies, waits for them, and re-layouts  1.88 us (1%)
    pallas_call x1, Pallas kernels, group_layer(): pl.pallas_call(functools.partial(layer_kernel, nz, bound), out_shape=jax....  139 us

profile of v8, /device:TPU:21, one launch (start us, length us, event | category | flops | bytes accessed | tf_op | source)
XLA Modules:
  0.0 141.3 jit_solution(10602981008669485912)
XLA Ops:
  0.0 139.4 %shard_map.64 = bf16[128,2048]{1,0:T(8,128)(2,1)} custom-call(bf16[128,2048]{1,0:T(8,128)(2,1)} %tok_hbm.1, s32[8,128]{1,0:T(8,128)} %bitcast.2, f32[8,128]{1,0:T(8,128)} %bitcast.3, s32[16,9]{1,0:T(8,128)} %slot_hbm.1, bf16[1,9,2048,768]{3,2,1,0:T(8,128)(2,1)} %up_hbm.1, bf16[1,9,768,2048]{3,2,1,0:T(8,128)(2,1)} %down_hbm.1), custom_call_target="tpu_custom_call" | custom-call | tf_op jit(solution)/shard_map/pallas_call | solution.py:504
  139.4 1.9 %copy.8 = bf16[128,2048]{1,0:T(8,128)(2,1)} copy(bf16[128,2048]{1,0:T(8,128)(2,1)} %shard_map.64) | data formatting | bytes 1048576

commit v9 on v7

--- a/solution.py
+++ b/solution.py
@@ -65,8 +65,8 @@
         return pltpu.make_async_remote_copy(src_ref=src, dst_ref=dst, send_sem=send, recv_sem=recv,
                                             device_id=dev, device_id_type=MESH)
 
-    def weight_copies(step):
-        buf, slot = step % W_DEPTH, step % n_slot
+    def weight_copies(slot):
+        buf = slot % W_DEPTH
         return (pltpu.make_async_copy(up_hbm.at[0, slot], up_buf.at[buf], w_sem.at[0, buf]),
                 pltpu.make_async_copy(down_hbm.at[0, slot], down_buf.at[buf], w_sem.at[1, buf]))
 
@@ -138,8 +138,8 @@
         for c in range(AG_CHUNKS):
             sib_copy(0, 0, c, core).start()
 
-    for step in range(W_DEPTH):
-        for copy in weight_copies(step):
+    for slot in range(W_DEPTH):
+        for copy in weight_copies(slot):
             copy.start()
 
     lane = lax.broadcasted_iota(jnp.int32, (cap, n_exp), 1)
@@ -287,10 +287,13 @@
         return remote(x_buf.at[slot, other], o_sib.at[slot], o_send.at[slot], o_recv.at[slot], device(z, other))
 
     def experts(slot, batch):
-        step = batch * n_slot + slot
-        buf = step % W_DEPTH
-        for copy in weight_copies(step):
-            copy.wait()
+        buf = slot % W_DEPTH
+
+        @pl.when((batch == 0) | (slot < n_slot - W_DEPTH))
+        def _():
+            for copy in weight_copies(slot):
+                copy.wait()
+
         x = x_buf[slot, batch].reshape(nz * cap, d_model)
         hidden = jax.nn.gelu(jnp.dot(x, up_buf[buf], preferred_element_type=F32), approximate=True).astype(BF16)
         for c in range(RS_CHUNKS):
@@ -302,9 +305,11 @@
         def _():
             o_copy(slot).start()
 
-        @pl.when(step + W_DEPTH < 2 * n_slot)
-        def _():
-            for copy in weight_copies(step + W_DEPTH):
+        following = slot + W_DEPTH if batch == 0 else slot - W_DEPTH
+
+        @pl.when((following >= 0) & (following < n_slot))
+        def _():
+            for copy in weight_copies(following):
                 copy.start()
 
     @pl.loop(0, n_slot)
@@ -427,12 +432,13 @@
                 second_pair(hop - 1)
 
     @pl.loop(0, n_slot)
-    def _(slot):
-        experts(slot, 1)
-
-        @pl.when((core == 0) & (slot < items - first - RS_CHUNKS))
-        def _():
-            later_item(first + RS_CHUNKS + slot)
+    def _(i):
+        experts(n_slot - 1 - i, 1)
+        n = items - n_slot + i
+
+        @pl.when((core == 0) & (n >= first + RS_CHUNKS))
+        def _():
+            later_item(n)
 
     start_chains(1)
 

time: 133 us -> 136 us (1.023)
  Pallas kernels: 131 us -> 134 us
    pallas_call x1, Pallas kernels: 131 us -> 134 us  [group_layer(): pl.pallas_call(functools.partial(layer_kernel, nz, bound), out_shape=jax....]
where the time goes in v9:
time: 136 us
  Pallas kernels  134 us (99%)
  local copies, waits for them, and re-layouts  1.88 us (1%)
    pallas_call x1, Pallas kernels, group_layer(): pl.pallas_call(functools.partial(layer_kernel, nz, bound), out_shape=jax....  134 us

profile of v9, /device:TPU:21, one launch (start us, length us, event | category | flops | bytes accessed | tf_op | source)
XLA Modules:
  0.0 135.8 jit_solution(1857166164837510345)
XLA Ops:
  0.0 133.9 %shard_map.64 = bf16[128,2048]{1,0:T(8,128)(2,1)} custom-call(bf16[128,2048]{1,0:T(8,128)(2,1)} %tok_hbm.1, s32[8,128]{1,0:T(8,128)} %bitcast.2, f32[8,128]{1,0:T(8,128)} %bitcast.3, s32[16,9]{1,0:T(8,128)} %slot_hbm.1, bf16[1,9,2048,768]{3,2,1,0:T(8,128)(2,1)} %up_hbm.1, bf16[1,9,768,2048]{3,2,1,0:T(8,128)(2,1)} %down_hbm.1), custom_call_target="tpu_custom_call" | custom-call | tf_op jit(solution)/shard_map/pallas_call | solution.py:513
  133.9 1.9 %copy.8 = bf16[128,2048]{1,0:T(8,128)(2,1)} copy(bf16[128,2048]{1,0:T(8,128)(2,1)} %shard_map.64) | data formatting | bytes 1048576

commit v10 on v7

--- a/solution.py
+++ b/solution.py
@@ -14,7 +14,7 @@
 W_DEPTH = 4
 AG_CHUNKS = 4
 RS_CHUNKS = 4
-AG2_LATE = (((3, 0), (3, 1)), ((3, 2), (3, 3)), ((4, 0), (4, 1)), (), ())
+AG2_LATE = (((3, 2), (3, 3)), ((4, 0), (4, 1)), (), (), ())
 AG2_HOP = 3
 
 
@@ -311,7 +311,7 @@
     def _(slot):
         experts(slot, 0)
 
-        @pl.when((core == 1) & (slot < 2 * AG_CHUNKS))
+        @pl.when(core == 1)
         def _():
             hop, n = 1 + slot // AG_CHUNKS, slot % AG_CHUNKS
             for d in range(2):
@@ -319,6 +319,11 @@
                 ag_arrival(d, hop, c).wait_recv()
                 ag_copy(d, hop + 1, c).start()
                 sib_copy(d, hop, c, core).start()
+
+    @pl.when(core == 1)
+    def _():
+        for n in range(n_slot - 2 * AG_CHUNKS, 2):
+            pass_on(half - 1, n)
 
     def from_sibling_o():
         @pl.loop(0, n_slot)

time: 133 us -> 135 us (1.015)
  Pallas kernels: 131 us -> 133 us
    pallas_call x1, Pallas kernels: 131 us -> 133 us  [group_layer(): pl.pallas_call(functools.partial(layer_kernel, nz, bound), out_shape=jax....]
where the time goes in v10:
time: 135 us; the launch traced here: 134 us
  Pallas kernels  133 us (99%)
  local copies, waits for them, and re-layouts  1.88 us (1%)
    pallas_call x1, Pallas kernels, group_layer(): pl.pallas_call(functools.partial(layer_kernel, nz, bound), out_shape=jax....  133 us

profile of v10, /device:TPU:21, one launch (start us, length us, event | category | flops | bytes accessed | tf_op | source)
XLA Modules:
  0.0 134.4 jit_solution(13369735756553647214)
XLA Ops:
  0.0 132.6 %shard_map.64 = bf16[128,2048]{1,0:T(8,128)(2,1)} custom-call(bf16[128,2048]{1,0:T(8,128)(2,1)} %tok_hbm.1, s32[8,128]{1,0:T(8,128)} %bitcast.2, f32[8,128]{1,0:T(8,128)} %bitcast.3, s32[16,9]{1,0:T(8,128)} %slot_hbm.1, bf16[1,9,2048,768]{3,2,1,0:T(8,128)(2,1)} %up_hbm.1, bf16[1,9,768,2048]{3,2,1,0:T(8,128)(2,1)} %down_hbm.1), custom_call_target="tpu_custom_call" | custom-call | tf_op jit(solution)/shard_map/pallas_call | solution.py:512
  132.6 1.9 %copy.8 = bf16[128,2048]{1,0:T(8,128)(2,1)} copy(bf16[128,2048]{1,0:T(8,128)(2,1)} %shard_map.64) | data formatting | bytes 1048576

commit v11 on v7

--- a/solution.py
+++ b/solution.py
@@ -14,7 +14,7 @@
 W_DEPTH = 4
 AG_CHUNKS = 4
 RS_CHUNKS = 4
-AG2_LATE = (((3, 0), (3, 1)), ((3, 2), (3, 3)), ((4, 0), (4, 1)), (), ())
+AG2_LATE = (((2, 3), (3, 0), (3, 1)), ((3, 2), (3, 3)), ((4, 0), (4, 1)), (), ())
 AG2_HOP = 3
 
 
@@ -311,9 +311,9 @@
     def _(slot):
         experts(slot, 0)
 
-        @pl.when((core == 1) & (slot < 2 * AG_CHUNKS))
-        def _():
-            hop, n = 1 + slot // AG_CHUNKS, slot % AG_CHUNKS
+        @pl.when((core == 1) & (slot >= 1) & (slot < 2 * AG_CHUNKS))
+        def _():
+            hop, n = 1 + (slot - 1) // AG_CHUNKS, (slot - 1) % AG_CHUNKS
             for d in range(2):
                 c = n if d == 0 else AG_CHUNKS - 1 - n
                 ag_arrival(d, hop, c).wait_recv()

time: 133 us -> 135 us (1.015)
  Pallas kernels: 131 us -> 133 us
    pallas_call x1, Pallas kernels: 131 us -> 133 us  [group_layer(): pl.pallas_call(functools.partial(layer_kernel, nz, bound), out_shape=jax....]
where the time goes in v11:
time: 135 us
  Pallas kernels  133 us (99%)
  local copies, waits for them, and re-layouts  1.88 us (1%)
    pallas_call x1, Pallas kernels, group_layer(): pl.pallas_call(functools.partial(layer_kernel, nz, bound), out_shape=jax....  133 us

profile of v11, /device:TPU:21, one launch (start us, length us, event | category | flops | bytes accessed | tf_op | source)
XLA Modules:
  0.0 134.6 jit_solution(4788272914558326182)
XLA Ops:
  0.0 132.7 %shard_map.64 = bf16[128,2048]{1,0:T(8,128)(2,1)} custom-call(bf16[128,2048]{1,0:T(8,128)(2,1)} %tok_hbm.1, s32[8,128]{1,0:T(8,128)} %bitcast.2, f32[8,128]{1,0:T(8,128)} %bitcast.3, s32[16,9]{1,0:T(8,128)} %slot_hbm.1, bf16[1,9,2048,768]{3,2,1,0:T(8,128)(2,1)} %up_hbm.1, bf16[1,9,768,2048]{3,2,1,0:T(8,128)(2,1)} %down_hbm.1), custom_call_target="tpu_custom_call" | custom-call | tf_op jit(solution)/shard_map/pallas_call | solution.py:507
  132.7 1.9 %copy.8 = bf16[128,2048]{1,0:T(8,128)(2,1)} copy(bf16[128,2048]{1,0:T(8,128)(2,1)} %shard_map.64) | data formatting | bytes 1048576
